TPU v7x, 32 devices: a whole 2x2x4 slice. The times are simulated.
32 devices in a mesh: gx: 4 (over z), gy: 8 (over y, x, core).
Axes of the slice: x: 2, y: 2, z: 4, core: 2. Of those that a mesh axis runs over, the one named last changes fastest.
Arguments:
- gradient: float32 [32, 2048], P('gx', 'gy'), may hold values from -6 to 6
- warm_start: float32 [32, 2048], P('gx', 'gy'), may hold values from -3 to 3
- viscosity: float32 [32, 32, 2048], P(None, 'gx', 'gy'), may hold values from 1 to 10
- friction_coef: float32 [32, 2048], P('gx', 'gy'), may hold values from 0.5 to 5
- slide_dir: float32 [2, 32, 2048], P(None, 'gx', 'gy'), may hold values from -4 to 4
- obs_weight: float32 [32, 2048], P('gx', 'gy'), may hold values from 0.5 to 2
- ice_mask: int32 [32, 2048], P('gx', 'gy'), may hold values 0 or 1
- grounded: int32 [32, 2048], P('gx', 'gy'), may hold values 0 or 1
Outputs:
- solution: float32 [32, 2048], P('gx', 'gy')
- residual: float32 [32, 2048], P('gx', 'gy')
All inputs are finite; a program needn't handle non-finite values. No bound on the sum of `ice_mask` or of `grounded` on one device may be relied on, other than what follows from the above.
Results may differ from a plain program's by a relative error of at most 0.00075.
Values sent between devices are 32-bit elements; how exact they have to be, the bound alone decides.
No kernel may reach another device: no remote copies, remote signals or barrier semaphores. Data moves between devices by JAX's collectives and lax.ppermute only.
A program may use at most 128 MiB of HBM per device.

v0:
```python
import jax
import jax.numpy as jnp
from jax import lax
from jax.sharding import PartitionSpec as P

ITERS = 2


vert_coupling = 128.0
sink_rate = 0.0625
bed_drag = 0.5
offset_weight = 0.0019
cross_share = 0.5
reg_gamma = 0.02
reg_smooth = 1.0
diag_scale = 0.003
neighbour_offsets = [
    (step_z, step_x, step_y)
    for step_z in (-1, 0, 1)
    for step_x in (-1, 0, 1)
    for step_y in (-1, 0, 1)
    if step_x != 0 or step_y != 0
]


def extended(block, sides, width):
    for axis, dim in sides:
        count = lax.axis_size(axis)
        forward = [(i, i + 1) for i in range(count - 1)]
        backward = [(target, source) for source, target in forward]
        low = lax.ppermute(
            lax.slice_in_dim(block, block.shape[dim] - width, None, axis=dim), axis, forward
        )
        high = lax.ppermute(lax.slice_in_dim(block, 0, width, axis=dim), axis, backward)
        block = jnp.concatenate([low, block, high], axis=dim)
    return block


def couple(field_ext, eta_ext):
    levels = eta_ext.shape[0]
    span_x = eta_ext.shape[1] - 2
    span_y = eta_ext.shape[2] - 2
    padded_field = jnp.pad(field_ext, ((0, 0), (1, 1), (0, 0), (0, 0)))
    padded_eta = jnp.pad(eta_ext, ((1, 1), (0, 0), (0, 0)))
    center = eta_ext[:, 1 : 1 + span_x, 1 : 1 + span_y]
    along_one = jnp.zeros((levels, span_x, span_y), jnp.float32)
    along_two = jnp.zeros((levels, span_x, span_y), jnp.float32)
    for step_z, step_x, step_y in neighbour_offsets:
        near_eta = padded_eta[
            1 + step_z : 1 + step_z + levels,
            1 + step_x : 1 + step_x + span_x,
            1 + step_y : 1 + step_y + span_y,
        ]
        weight = (
            offset_weight / (abs(step_x) + abs(step_y) + abs(step_z)) * 0.5 * (center + near_eta)
        )
        near_field = padded_field[
            :,
            1 + step_z : 1 + step_z + levels,
            1 + step_x : 1 + step_x + span_x,
            1 + step_y : 1 + step_y + span_y,
        ]
        along_one = along_one + weight * near_field[0]
        along_two = along_two + weight * near_field[1]
        if step_x != 0 and step_y != 0:
            twist_weight = cross_share * step_x * step_y * weight
            along_one = along_one + twist_weight * near_field[1]
            along_two = along_two + twist_weight * near_field[0]
    return jnp.stack([along_one, along_two])


def tridiagonal(link_weights, diagonal, rhs_cols):
    levels = diagonal.shape[0]
    pivot_value = diagonal[0]
    ratios = [-link_weights[0] / pivot_value]
    partial_value = [rhs_cols[:, 0] / pivot_value]
    for layer_index in range(1, levels):
        pivot_value = diagonal[layer_index] + link_weights[layer_index - 1] * ratios[-1]
        partial_value.append(
            (rhs_cols[:, layer_index] + link_weights[layer_index - 1] * partial_value[-1])
            / pivot_value
        )
        if layer_index < levels - 1:
            ratios.append(-link_weights[layer_index] / pivot_value)
    result = [partial_value[-1]]
    for layer_index in range(levels - 2, -1, -1):
        result.insert(0, partial_value[layer_index] - ratios[layer_index] * result[0])
    return jnp.stack(result, axis=1)


def responses(viscosity, friction):
    levels = viscosity.shape[0]
    link_weights = vert_coupling * 0.5 * (viscosity[:-1] + viscosity[1:])
    zero_layer = jnp.zeros_like(viscosity[:1])
    diagonal = (
        jnp.concatenate([zero_layer, link_weights])
        + jnp.concatenate([link_weights, zero_layer])
        + sink_rate * viscosity
    )
    diagonal = diagonal.at[0].add(bed_drag * friction)
    unit_rhs = jnp.zeros((2,) + viscosity.shape, jnp.float32)
    unit_rhs = unit_rhs.at[0, 0].set(1.0).at[1, levels - 1].set(1.0)
    solved = tridiagonal(link_weights, diagonal, unit_rhs)
    return (solved[0], solved[1])


def regularize(centre_ext):
    middle = centre_ext[1:-1, 1:-1]
    beside_all = (
        centre_ext[2:, 1:-1] + centre_ext[:-2, 1:-1] + centre_ext[1:-1, 2:] + centre_ext[1:-1, :-2]
    )
    return reg_gamma * (middle + reg_smooth * (4.0 * middle - beside_all))


def residual_dot(residual, precond):
    return lax.psum(jnp.sum(residual * precond), ("gx", "gy"))


def on_device(
    gradient, warm_start, viscosity, friction_coef, slide_dir, obs_weight, ice_mask, grounded
):
    ice_float = ice_mask.astype(jnp.float32)
    ground_float = grounded.astype(jnp.float32)
    friction = ground_float * friction_coef
    source = (ice_float * ground_float * friction_coef)[None] * slide_dir
    obs = ice_float * obs_weight
    inverse_diag = 1.0 / (
        reg_gamma * (1.0 + 4.0 * reg_smooth)
        + diag_scale * ice_float * ground_float * friction_coef * friction_coef
    )
    viscosity_wide = extended(viscosity, (("gx", 1), ("gy", 2)), 2)
    columns = jnp.concatenate([source, obs[None], friction[None]], axis=0)
    column_wide = extended(columns, (("gx", 1), ("gy", 2)), 2)
    safe_eta = jnp.where(viscosity_wide > 0.0, viscosity_wide, 1.0)
    bottom_wide, top_wide = responses(safe_eta, column_wide[3])
    bottom_inner = bottom_wide[:, 1:-1, 1:-1]
    top_inner = top_wide[:, 1:-1, 1:-1]
    bottom_own = bottom_wide[:, 2:-2, 2:-2]
    top_own = top_wide[:, 2:-2, 2:-2]

    def hessian(direction):
        wide_dir = extended(direction, (("gx", 0), ("gy", 1)), 2)
        spread = column_wide[:2] * wide_dir[None]
        first_state = bottom_wide[None] * spread[:, None]
        coupled = couple(first_state, viscosity_wide)
        surface = spread[:, 1:-1, 1:-1] * bottom_inner[-1][None] + jnp.sum(
            top_inner[None] * coupled, axis=1
        )
        traction = column_wide[2, 1:-1, 1:-1][None] * surface
        second_state = top_inner[None] * traction[:, None]
        coupled_back = couple(second_state, viscosity_wide[:, 1:-1, 1:-1])
        basal_part = traction[:, 1:-1, 1:-1] * top_own[0][None] + jnp.sum(
            bottom_own[None] * coupled_back, axis=1
        )
        return jnp.sum(source * basal_part, axis=0) + regularize(wide_dir[1:-1, 1:-1])

    solution = warm_start
    residual = gradient - hessian(warm_start)
    precond = inverse_diag * residual
    direction = precond
    norm_now = residual_dot(residual, precond)
    for iteration in range(ITERS):
        image_vec = hessian(direction)
        step_size = norm_now / lax.psum(jnp.sum(direction * image_vec), ("gx", "gy"))
        solution = solution + step_size * direction
        residual = residual - step_size * image_vec
        precond = inverse_diag * residual
        norm_next = residual_dot(residual, precond)
        direction = precond + norm_next / norm_now * direction
        norm_now = norm_next
    return (solution, residual)


def solution(mesh):
    return jax.shard_map(
        on_device,
        mesh=mesh,
        in_specs=(
            P("gx", "gy"),
            P("gx", "gy"),
            P(None, "gx", "gy"),
            P("gx", "gy"),
            P(None, "gx", "gy"),
            P("gx", "gy"),
            P("gx", "gy"),
            P("gx", "gy"),
        ),
        out_specs=(P("gx", "gy"), P("gx", "gy")),
        check_vma=False,
    )
```

profile of v0, /device:TPU:0, one launch (start us, length us, event | category | flops | bytes accessed | tf_op | source)
XLA Modules:
  0.0 328.0 jit_solution(8467789932187685515)
XLA Ops:
  1.4 4.9 %collective-permute-start.4 = (f32[2,256]{1,0:T(2,128)S(1)}, f32[2,256]{1,0:T(2,128)S(1)}, u32[]{:S(2)}, u32[]{:S(2)}) collective-permute-start(f32[2,256]{1,0:T(2,128)S(1)} %get-tuple-element.248), channel_id=1, source_target_pairs={{0,8},{8,16},{16,24},{1,9},{9,17},{17,25},{2,10},{10,18},{18,26},{... | collective-permute-start | bytes 6152 | tf_op jit(solution)/shard_map/ppermute | solution.py:31
  9.2 4.7 %collective-permute-start = (f32[4,2,256]{2,1,0:T(2,128)S(1)}, f32[4,2,256]{2,1,0:T(2,128)S(1)}, u32[]{:S(2)}, u32[]{:S(2)}) collective-permute-start(f32[4,2,256]{2,1,0:T(2,128)S(1)} %get-tuple-element.233), channel_id=1, source_target_pairs={{0,8},{8,16},{16,24},{1,9},{9,17},{17,25},{2,10},{10,18},{18,26},{... | collective-permute-start | bytes 24584 | tf_op jit(solution)/shard_map/ppermute | solution.py:31
  16.2 4.5 %collective-permute-start.8 = (f32[32,2,256]{2,1,0:T(2,128)S(1)}, f32[32,2,256]{2,1,0:T(2,128)S(1)}, u32[]{:S(2)}, u32[]{:S(2)}) collective-permute-start(f32[32,2,256]{2,1,0:T(2,128)S(1)} %get-tuple-element.229), channel_id=1, source_target_pairs={{0,8},{8,16},{16,24},{1,9},{9,17},{17,25},{2,10},{10,18},{18,26},{... | collective-permute-start | bytes 196616 | tf_op jit(solution)/shard_map/ppermute | solution.py:31
  25.6 4.8 %collective-permute-start.2 = (f32[4,12,2]{2,1,0:T(8,128)S(1)}, f32[4,12,2]{2,1,0:T(8,128)S(1)}, u32[]{:S(2)}, u32[]{:S(2)}) collective-permute-start(f32[4,12,2]{2,1,0:T(8,128)S(1)} %get-tuple-element.231), channel_id=1, source_target_pairs={{0,1},{1,2},{2,3},{3,4},{4,5},{5,6},{6,7},{8,9},{9,10},{10,11},{11... | collective-permute-start | bytes 1160 | tf_op jit(solution)/shard_map/ppermute | solution.py:31
  36.7 4.5 %collective-permute-start.10 = (f32[32,12,2]{2,1,0:T(8,128)S(1)}, f32[32,12,2]{2,1,0:T(8,128)S(1)}, u32[]{:S(2)}, u32[]{:S(2)}) collective-permute-start(f32[32,12,2]{2,1,0:T(8,128)S(1)} %get-tuple-element.225), channel_id=1, source_target_pairs={{0,1},{1,2},{2,3},{3,4},{4,5},{5,6},{6,7},{8,9},{9,10},{10,11},{11... | collective-permute-start | bytes 9224 | tf_op jit(solution)/shard_map/ppermute | solution.py:31
  51.7 9.6 %fusion.241 = (f32[1,32,10,258]{3,2,1,0:T(8,128)}, f32[32,10,258]{2,1,0:T(8,128)S(1)}, f32[32,10,258]{2,1,0:T(8,128)S(1)}, f32[32,10,258]{2,1,0:T(8,128)S(1)}, f...) fusion(f32[2,32,12,260]{3,2,1,0:T(8,128)S(1)} %broadcast_multip, ...), kind=kLoop, calls=%fused_computation.521 | loop fusion | flops 10815360 | bytes 27130368 | tf_op jit(solution)/shard_map/stack | solution.py:69
  61.4 9.7 %fusion.242 = f32[1,32,10,258]{3,2,1,0:T(8,128)} fusion(f32[32,10,258]{2,1,0:T(8,128)} %get-tuple-element.96, f32[32,10,258]{2,1,0:T(8,128)} %get-tuple-element.95, f32[32,10,258]{2,1,0:T(8,128)} %get-tuple-element.94, f32[32,10,258]{2,1,0:T(8,128)} %get-tuple-element.93, f32[32,10,258]{2,1,0:T(8,128)} %get-tuple-element.92, ...), kind=kLoop, calls=%fused_computation.522 | loop fusion | flops 7843200 | bytes 22459392 | tf_op jit(solution)/shard_map/stack | solution.py:69
  74.4 4.4 %fusion.518 = (f32[1,32,8,256]{3,2,1,0:T(8,128)}, f32[32,8,256]{2,1,0:T(8,128)}, f32[32,8,256]{2,1,0:T(8,128)}, f32[32,8,256]{2,1,0:T(8,128)}, f32[32,8,256]{2,1...) fusion(f32[2,32,10,258]{3,2,1,0:T(8,128)S(1)} %broadcast_multip, ...), kind=kLoop, calls=%fused_computation.1103 | loop fusion | flops 8716288 | bytes 13500416 | tf_op jit(solution)/shard_map/stack | solution.py:69
  78.9 4.5 %fusion.515 = f32[1,32,8,256]{3,2,1,0:T(8,128)} fusion(f32[32,8,256]{2,1,0:T(8,128)} %get-tuple-element.71, f32[32,8,256]{2,1,0:T(8,128)} %get-tuple-element.70, f32[32,8,256]{2,1,0:T(8,128)} %get-tuple-element.69, f32[32,8,256]{2,1,0:T(8,128)} %get-tuple-element.68, f32[2,32,10,258]{3,2,1,0:T(8,128)S(1)} %broadcast_multiply_fusion.4, ...), kind=kLoop, calls=%fused_computation.1100 | loop fusion | flops 6619136 | bytes 11141120 | tf_op jit(solution)/shard_map/stack | solution.py:69
  87.3 4.5 %collective-permute-start.12 = (f32[2,256]{1,0:T(2,128)S(1)}, f32[2,256]{1,0:T(2,128)S(1)}, u32[]{:S(2)}, u32[]{:S(2)}) collective-permute-start(f32[2,256]{1,0:T(2,128)S(1)} %get-tuple-element.246), channel_id=1, source_target_pairs={{0,8},{8,16},{16,24},{1,9},{9,17},{17,25},{2,10},{10,18},{18,26},{... | collective-permute-start | bytes 6152 | tf_op jit(solution)/shard_map/ppermute | solution.py:31
  93.2 4.2 %collective-permute-done.13 = f32[2,256]{1,0:T(2,128)S(1)} collective-permute-done((f32[2,256]{1,0:T(2,128)S(1)}, f32[2,256]{1,0:T(2,128)S(1)}, u32[]{:S(2)}, u32[]{:S(2)}) %collective-permute-start.13) | collective-permute-done | bytes 2080 | tf_op jit(solution)/shard_map/ppermute | solution.py:34
  97.4 6.6 %collective-permute-start.14 = (f32[12,2]{1,0:T(8,128)S(1)}, f32[12,2]{1,0:T(8,128)S(1)}, u32[]{:S(2)}, u32[]{:S(2)}) collective-permute-start(f32[12,2]{1,0:T(8,128)S(1)} %get-tuple-element.237), channel_id=1, source_target_pairs={{0,1},{1,2},{2,3},{3,4},{4,5},{5,6},{6,7},{8,9},{9,10},{10,11},{11... | collective-permute-start | bytes 296 | tf_op jit(solution)/shard_map/ppermute | solution.py:31
  111.3 8.6 %fusion.244 = f32[1,32,10,258]{3,2,1,0:T(8,128)} fusion(f32[32,10,258]{2,1,0:T(8,128)} %get-tuple-element.96, f32[32,10,258]{2,1,0:T(8,128)} %get-tuple-element.95, f32[32,10,258]{2,1,0:T(8,128)} %get-tuple-element.94, f32[32,10,258]{2,1,0:T(8,128)} %get-tuple-element.93, f32[32,10,258]{2,1,0:T(8,128)} %get-tuple-element.92, ...), kind=kLoop, calls=%fused_computation.524 | loop fusion | flops 7843200 | bytes 22459392 | tf_op jit(solution)/shard_map/stack | solution.py:69
  120.0 8.6 %fusion.243 = f32[1,32,10,258]{3,2,1,0:T(8,128)} fusion(f32[32,10,258]{2,1,0:T(8,128)} %get-tuple-element.96, f32[32,10,258]{2,1,0:T(8,128)} %get-tuple-element.95, f32[32,10,258]{2,1,0:T(8,128)} %get-tuple-element.94, f32[32,10,258]{2,1,0:T(8,128)} %get-tuple-element.93, f32[32,10,258]{2,1,0:T(8,128)} %get-tuple-element.92, ...), kind=kLoop, calls=%fused_computation.523 | loop fusion | flops 7843200 | bytes 22459392 | tf_op jit(solution)/shard_map/stack | solution.py:69
  131.1 4.5 %fusion.516 = f32[1,32,8,256]{3,2,1,0:T(8,128)} fusion(f32[32,8,256]{2,1,0:T(8,128)} %get-tuple-element.71, f32[32,8,256]{2,1,0:T(8,128)} %get-tuple-element.70, f32[32,8,256]{2,1,0:T(8,128)} %get-tuple-element.69, f32[32,8,256]{2,1,0:T(8,128)} %get-tuple-element.68, f32[2,32,10,258]{3,2,1,0:T(8,128)S(1)} %broadcast_multiply_fusion.2, ...), kind=kLoop, calls=%fused_computation.1101 | loop fusion | flops 6619136 | bytes 11141120 | tf_op jit(solution)/shard_map/stack | solution.py:69
  135.6 4.5 %fusion.519 = f32[1,32,8,256]{3,2,1,0:T(8,128)} fusion(f32[32,8,256]{2,1,0:T(8,128)} %get-tuple-element.71, f32[2,32,10,258]{3,2,1,0:T(8,128)S(1)} %broadcast_multiply_fusion.2, f32[32,8,256]{2,1,0:T(8,128)} %get-tuple-element.70, f32[32,8,256]{2,1,0:T(8,128)} %get-tuple-element.69, f32[32,8,256]{2,1,0:T(8,128)} %get-tuple-element.68, ...), kind=kLoop, calls=%fused_computation.1104 | loop fusion | flops 6619136 | bytes 11141120 | tf_op jit(solution)/shard_map/stack | solution.py:69
  143.7 43.1 %all-reduce.10 = (f32[]{:T(128)}, f32[]{:T(128)}) all-reduce(f32[]{:T(128)} %get-tuple-element.39, f32[]{:T(128)} %get-tuple-element.38), channel_id=1, replica_groups=mesh['gx'=4,'gy'=8] {'gx','gy'}, use_global_device_ids=true, to_apply=%region_4.5 | all-reduce | flops 2 | bytes 16 | tf_op jit(solution)/shard_map/psum | solution.py:116
  190.1 39.1 %psum.30 = f32[]{:T(128)} all-reduce(f32[]{:T(128)} %get-tuple-element.44), channel_id=1, replica_groups=mesh['gx'=4,'gy'=8] {'gx','gy'}, use_global_device_ids=true, to_apply=%region_11.12 | all-reduce | flops 1 | bytes 8 | tf_op jit(solution)/shard_map/psum | solution.py:116
  236.6 4.2 %collective-permute-done.17 = f32[2,256]{1,0:T(2,128)S(1)} collective-permute-done((f32[2,256]{1,0:T(2,128)S(1)}, f32[2,256]{1,0:T(2,128)S(1)}, u32[]{:S(2)}, u32[]{:S(2)}) %collective-permute-start.17) | collective-permute-done | bytes 2080 | tf_op jit(solution)/shard_map/ppermute | solution.py:34
  243.6 4.0 %collective-permute-done.19 = f32[12,2]{1,0:T(8,128)S(1)} collective-permute-done((f32[12,2]{1,0:T(8,128)S(1)}, f32[12,2]{1,0:T(8,128)S(1)}, u32[]{:S(2)}, u32[]{:S(2)}) %collective-permute-start.19) | collective-permute-done | bytes 128 | tf_op jit(solution)/shard_map/ppermute | solution.py:34
  250.5 8.8 %fusion.246 = f32[1,32,10,258]{3,2,1,0:T(8,128)} fusion(f32[32,10,258]{2,1,0:T(8,128)} %get-tuple-element.96, f32[32,10,258]{2,1,0:T(8,128)} %get-tuple-element.95, f32[32,10,258]{2,1,0:T(8,128)} %get-tuple-element.94, f32[32,10,258]{2,1,0:T(8,128)} %get-tuple-element.93, f32[32,10,258]{2,1,0:T(8,128)} %get-tuple-element.92, ...), kind=kLoop, calls=%fused_computation.526 | loop fusion | flops 7843200 | bytes 22003200 | tf_op jit(solution)/shard_map/stack | solution.py:69
  259.3 8.6 %fusion.245 = f32[1,32,10,258]{3,2,1,0:T(8,128)} fusion(f32[32,10,258]{2,1,0:T(8,128)} %get-tuple-element.96, f32[32,10,258]{2,1,0:T(8,128)} %get-tuple-element.95, f32[32,10,258]{2,1,0:T(8,128)} %get-tuple-element.94, f32[32,10,258]{2,1,0:T(8,128)} %get-tuple-element.93, f32[32,10,258]{2,1,0:T(8,128)} %get-tuple-element.92, ...), kind=kLoop, calls=%fused_computation.525 | loop fusion | flops 7843200 | bytes 22459392 | tf_op jit(solution)/shard_map/stack | solution.py:69
  271.3 4.1 %fusion.517 = f32[1,32,8,256]{3,2,1,0:T(8,128)} fusion(f32[32,8,256]{2,1,0:T(8,128)} %get-tuple-element.71, f32[32,8,256]{2,1,0:T(8,128)} %get-tuple-element.70, f32[32,8,256]{2,1,0:T(8,128)} %get-tuple-element.69, f32[32,8,256]{2,1,0:T(8,128)} %get-tuple-element.68, f32[2,32,10,258]{3,2,1,0:T(8,128)S(1)} %broadcast_multiply_fusion, ...), kind=kLoop, calls=%fused_computation.1102 | loop fusion | flops 6619136 | bytes 11141120 | tf_op jit(solution)/shard_map/stack | solution.py:69
  283.0 42.3 %psum.31 = f32[]{:T(128)} all-reduce(f32[]{:T(128)} %get-tuple-element.42), channel_id=1, replica_groups=mesh['gx'=4,'gy'=8] {'gx','gy'}, use_global_device_ids=true, to_apply=%region_16.17 | all-reduce | flops 1 | bytes 8 | tf_op jit(solution)/shard_map/psum | solution.py:164
  (270 shorter events, 74.2 us)
Async XLA Ops:
  1.4 19.4 %collective-permute-start.4 = (f32[2,256]{1,0:T(2,128)S(1)}, f32[2,256]{1,0:T(2,128)S(1)}, u32[]{:S(2)}, u32[]{:S(2)}) collective-permute-start(f32[2,256]{1,0:T(2,128)S(1)} %get-tuple-element.248), channel_id=1, source_target_pairs={{0,8},{8,16},{16,24},{1,9},{9,17},{17,25},{2,10},{10,18},{18,26},{... | collective-permute-start | bytes 6152 | tf_op jit(solution)/shard_map/ppermute | solution.py:31
  6.4 15.7 %collective-permute-start.5 = (f32[2,256]{1,0:T(2,128)S(1)}, f32[2,256]{1,0:T(2,128)S(1)}, u32[]{:S(2)}, u32[]{:S(2)}) collective-permute-start(f32[2,256]{1,0:T(2,128)S(1)} %get-tuple-element.249), channel_id=1, source_target_pairs={{8,0},{16,8},{24,16},{9,1},{17,9},{25,17},{10,2},{18,10},{26,18},{... | collective-permute-start | bytes 6152 | tf_op jit(solution)/shard_map/ppermute | solution.py:34
  8.4 132.9 %copy-start.48 = (f32[8,256]{1,0:T(8,128)}, f32[8,256]{1,0:T(8,128)S(1)}, u32[]{:S(2)}) copy-start(f32[8,256]{1,0:T(8,128)S(1)} %get-tuple-element.242) | copy-start | bytes 24580
  9.1 35.5 %copy-start.12 = (f32[32,8,256]{2,1,0:T(8,128)S(1)}, f32[32,8,256]{2,1,0:T(8,128)}, u32[]{:S(2)}) copy-start(f32[32,8,256]{2,1,0:T(8,128)} %param.16) | copy-start | bytes 786436
  9.2 15.0 %collective-permute-start = (f32[4,2,256]{2,1,0:T(2,128)S(1)}, f32[4,2,256]{2,1,0:T(2,128)S(1)}, u32[]{:S(2)}, u32[]{:S(2)}) collective-permute-start(f32[4,2,256]{2,1,0:T(2,128)S(1)} %get-tuple-element.233), channel_id=1, source_target_pairs={{0,8},{8,16},{16,24},{1,9},{9,17},{17,25},{2,10},{10,18},{18,26},{... | collective-permute-start | bytes 24584 | tf_op jit(solution)/shard_map/ppermute | solution.py:31
  13.8 11.7 %collective-permute-start.1 = (f32[4,2,256]{2,1,0:T(2,128)S(1)}, f32[4,2,256]{2,1,0:T(2,128)S(1)}, u32[]{:S(2)}, u32[]{:S(2)}) collective-permute-start(f32[4,2,256]{2,1,0:T(2,128)S(1)} %get-tuple-element.234), channel_id=1, source_target_pairs={{8,0},{16,8},{24,16},{9,1},{17,9},{25,17},{10,2},{18,10},{26,18},{... | collective-permute-start | bytes 24584 | tf_op jit(solution)/shard_map/ppermute | solution.py:34
  16.2 18.7 %collective-permute-start.8 = (f32[32,2,256]{2,1,0:T(2,128)S(1)}, f32[32,2,256]{2,1,0:T(2,128)S(1)}, u32[]{:S(2)}, u32[]{:S(2)}) collective-permute-start(f32[32,2,256]{2,1,0:T(2,128)S(1)} %get-tuple-element.229), channel_id=1, source_target_pairs={{0,8},{8,16},{16,24},{1,9},{9,17},{17,25},{2,10},{10,18},{18,26},{... | collective-permute-start | bytes 196616 | tf_op jit(solution)/shard_map/ppermute | solution.py:31
  20.8 14.7 %collective-permute-start.9 = (f32[32,2,256]{2,1,0:T(2,128)S(1)}, f32[32,2,256]{2,1,0:T(2,128)S(1)}, u32[]{:S(2)}, u32[]{:S(2)}) collective-permute-start(f32[32,2,256]{2,1,0:T(2,128)S(1)} %get-tuple-element.230), channel_id=1, source_target_pairs={{8,0},{16,8},{24,16},{9,1},{17,9},{25,17},{10,2},{18,10},{26,18},{... | collective-permute-start | bytes 196616 | tf_op jit(solution)/shard_map/ppermute | solution.py:34
  22.9 7.5 %collective-permute-start.6 = (f32[12,2]{1,0:T(8,128)S(1)}, f32[12,2]{1,0:T(8,128)S(1)}, u32[]{:S(2)}, u32[]{:S(2)}) collective-permute-start(f32[12,2]{1,0:T(8,128)S(1)} %get-tuple-element.239), channel_id=1, source_target_pairs={{0,1},{1,2},{2,3},{3,4},{4,5},{5,6},{6,7},{8,9},{9,10},{10,11},{11... | collective-permute-start | bytes 296 | tf_op jit(solution)/shard_map/ppermute | solution.py:31
  24.2 7.5 %collective-permute-start.7 = (f32[12,2]{1,0:T(8,128)S(1)}, f32[12,2]{1,0:T(8,128)S(1)}, u32[]{:S(2)}, u32[]{:S(2)}) collective-permute-start(f32[12,2]{1,0:T(8,128)S(1)} %get-tuple-element.240), channel_id=1, source_target_pairs={{1,0},{2,1},{3,2},{4,3},{5,4},{6,5},{7,6},{9,8},{10,9},{11,10},{12... | collective-permute-start | bytes 296 | tf_op jit(solution)/shard_map/ppermute | solution.py:34
  25.6 6.9 %collective-permute-start.2 = (f32[4,12,2]{2,1,0:T(8,128)S(1)}, f32[4,12,2]{2,1,0:T(8,128)S(1)}, u32[]{:S(2)}, u32[]{:S(2)}) collective-permute-start(f32[4,12,2]{2,1,0:T(8,128)S(1)} %get-tuple-element.231), channel_id=1, source_target_pairs={{0,1},{1,2},{2,3},{3,4},{4,5},{5,6},{6,7},{8,9},{9,10},{10,11},{11... | collective-permute-start | bytes 1160 | tf_op jit(solution)/shard_map/ppermute | solution.py:31
  30.4 4.3 %collective-permute-start.3 = (f32[4,12,2]{2,1,0:T(8,128)S(1)}, f32[4,12,2]{2,1,0:T(8,128)S(1)}, u32[]{:S(2)}, u32[]{:S(2)}) collective-permute-start(f32[4,12,2]{2,1,0:T(8,128)S(1)} %get-tuple-element.232), channel_id=1, source_target_pairs={{1,0},{2,1},{3,2},{4,3},{5,4},{6,5},{7,6},{9,8},{10,9},{11,10},{12... | collective-permute-start | bytes 1160 | tf_op jit(solution)/shard_map/ppermute | solution.py:34
  36.7 6.5 %collective-permute-start.10 = (f32[32,12,2]{2,1,0:T(8,128)S(1)}, f32[32,12,2]{2,1,0:T(8,128)S(1)}, u32[]{:S(2)}, u32[]{:S(2)}) collective-permute-start(f32[32,12,2]{2,1,0:T(8,128)S(1)} %get-tuple-element.225), channel_id=1, source_target_pairs={{0,1},{1,2},{2,3},{3,4},{4,5},{5,6},{6,7},{8,9},{9,10},{10,11},{11... | collective-permute-start | bytes 9224 | tf_op jit(solution)/shard_map/ppermute | solution.py:31
  41.2 3.4 %collective-permute-start.11 = (f32[32,12,2]{2,1,0:T(8,128)S(1)}, f32[32,12,2]{2,1,0:T(8,128)S(1)}, u32[]{:S(2)}, u32[]{:S(2)}) collective-permute-start(f32[32,12,2]{2,1,0:T(8,128)S(1)} %get-tuple-element.226), channel_id=1, source_target_pairs={{1,0},{2,1},{3,2},{4,3},{5,4},{6,5},{7,6},{9,8},{10,9},{11,10},{12... | collective-permute-start | bytes 9224 | tf_op jit(solution)/shard_map/ppermute | solution.py:34
  83.4 27.9 %copy-start.10 = (f32[32,10,258]{2,1,0:T(8,128)S(1)}, f32[32,10,258]{2,1,0:T(8,128)}, u32[]{:S(2)}) copy-start(f32[32,10,258]{2,1,0:T(8,128)} %copy-done.9) | copy-start | bytes 990724
  84.6 26.7 %copy-start.1 = (f32[32,10,258]{2,1,0:T(8,128)S(1)}, f32[32,10,258]{2,1,0:T(8,128)}, u32[]{:S(2)}) copy-start(f32[32,10,258]{2,1,0:T(8,128)} %copy-done) | copy-start | bytes 990724
  87.3 5.9 %collective-permute-start.12 = (f32[2,256]{1,0:T(2,128)S(1)}, f32[2,256]{1,0:T(2,128)S(1)}, u32[]{:S(2)}, u32[]{:S(2)}) collective-permute-start(f32[2,256]{1,0:T(2,128)S(1)} %get-tuple-element.246), channel_id=1, source_target_pairs={{0,8},{8,16},{16,24},{1,9},{9,17},{17,25},{2,10},{10,18},{18,26},{... | collective-permute-start | bytes 6152 | tf_op jit(solution)/shard_map/ppermute | solution.py:31
  91.9 5.5 %collective-permute-start.13 = (f32[2,256]{1,0:T(2,128)S(1)}, f32[2,256]{1,0:T(2,128)S(1)}, u32[]{:S(2)}, u32[]{:S(2)}) collective-permute-start(f32[2,256]{1,0:T(2,128)S(1)} %get-tuple-element.247), channel_id=1, source_target_pairs={{8,0},{16,8},{24,16},{9,1},{17,9},{25,17},{10,2},{18,10},{26,18},{... | collective-permute-start | bytes 6152 | tf_op jit(solution)/shard_map/ppermute | solution.py:34
  97.4 8.1 %collective-permute-start.14 = (f32[12,2]{1,0:T(8,128)S(1)}, f32[12,2]{1,0:T(8,128)S(1)}, u32[]{:S(2)}, u32[]{:S(2)}) collective-permute-start(f32[12,2]{1,0:T(8,128)S(1)} %get-tuple-element.237), channel_id=1, source_target_pairs={{0,1},{1,2},{2,3},{3,4},{4,5},{5,6},{6,7},{8,9},{9,10},{10,11},{11... | collective-permute-start | bytes 296 | tf_op jit(solution)/shard_map/ppermute | solution.py:31
  104.0 4.0 %collective-permute-start.15 = (f32[12,2]{1,0:T(8,128)S(1)}, f32[12,2]{1,0:T(8,128)S(1)}, u32[]{:S(2)}, u32[]{:S(2)}) collective-permute-start(f32[12,2]{1,0:T(8,128)S(1)} %get-tuple-element.238), channel_id=1, source_target_pairs={{1,0},{2,1},{3,2},{4,3},{5,4},{6,5},{7,6},{9,8},{10,9},{11,10},{12... | collective-permute-start | bytes 296 | tf_op jit(solution)/shard_map/ppermute | solution.py:34
  231.6 5.0 %collective-permute-start.16 = (f32[2,256]{1,0:T(2,128)S(1)}, f32[2,256]{1,0:T(2,128)S(1)}, u32[]{:S(2)}, u32[]{:S(2)}) collective-permute-start(f32[2,256]{1,0:T(2,128)S(1)} %get-tuple-element.244), channel_id=1, source_target_pairs={{0,8},{8,16},{16,24},{1,9},{9,17},{17,25},{2,10},{10,18},{18,26},{... | collective-permute-start | bytes 6152 | tf_op jit(solution)/shard_map/ppermute | solution.py:31
  235.3 5.5 %collective-permute-start.17 = (f32[2,256]{1,0:T(2,128)S(1)}, f32[2,256]{1,0:T(2,128)S(1)}, u32[]{:S(2)}, u32[]{:S(2)}) collective-permute-start(f32[2,256]{1,0:T(2,128)S(1)} %get-tuple-element.245), channel_id=1, source_target_pairs={{8,0},{16,8},{24,16},{9,1},{17,9},{25,17},{10,2},{18,10},{26,18},{... | collective-permute-start | bytes 6152 | tf_op jit(solution)/shard_map/ppermute | solution.py:34
  240.8 2.8 collective-permute-start.18
  242.1 5.6 %collective-permute-start.19 = (f32[12,2]{1,0:T(8,128)S(1)}, f32[12,2]{1,0:T(8,128)S(1)}, u32[]{:S(2)}, u32[]{:S(2)}) collective-permute-start(f32[12,2]{1,0:T(8,128)S(1)} %get-tuple-element.236), channel_id=1, source_target_pairs={{1,0},{2,1},{3,2},{4,3},{5,4},{6,5},{7,6},{9,8},{10,9},{11,10},{12... | collective-permute-start | bytes 296 | tf_op jit(solution)/shard_map/ppermute | solution.py:34
  (61 other events, 411.8 us)
where the time goes:
time: 330 us; the launch traced here: 328 us
  blocking collectives  125 us (38%)
  other arithmetic  112 us (34%)
  starting transfers between devices  54.2 us (16%)
  waiting for transfers between devices  18.6 us (6%)
  local copies, waits for them, and re-layouts  12.1 us (4%)
  between operations  6.23 us (2%)
    psum x2, blocking collectives, residual_dot(): return lax.psum(jnp.sum(residual * precond), ('gx', 'gy'))  82.2 us
    another operation x12, other arithmetic, couple(): return jnp.stack([along_one, along_two])  80.2 us
    psum x1, blocking collectives, on_device(): lax.psum(jnp.sum(direction * image_vec), ('gx', 'gy'))  42.3 us
    ppermute x10, starting transfers between devices, extended(): lax.ppermute(lax.slice_in_dim(block, block.shape[dim] - width, None, axis...  40.8 us
    ppermute x10, waiting for transfers between devices, extended(): lax.ppermute(lax.slice_in_dim(block, 0, width, axis=dim), axis, backward)  18.6 us
    ppermute x10, starting transfers between devices, extended(): lax.ppermute(lax.slice_in_dim(block, 0, width, axis=dim), axis, backward)  13.3 us
  transfers between devices with their start and end apart: 20, of which 6 were waited for; matrix products, arithmetic and copies ran while one was open for 2% of the time, Pallas kernels for 0%

commit v1 on v0

v1 whole, which is shorter than its diff:
```python
import jax
import jax.numpy as jnp
from jax import lax
from jax.experimental import pallas as pl
from jax.experimental.pallas import tpu as pltpu
from jax.sharding import PartitionSpec as P

vert_coupling = 128.0
sink_rate = 0.0625
bed_drag = 0.5
offset_weight = 0.0019
cross_share = 0.5
reg_gamma = 0.02
reg_smooth = 1.0
diag_scale = 0.003

HALO = 6
FIELDS = 7


def round_up(value, step):
    return -(-value // step) * step


def moved(block, step_x, step_y):
    if step_y:
        block = pltpu.roll(block, (-step_y) % block.shape[1], 1)
    if step_x:
        block = pltpu.roll(block, (-step_x) % block.shape[0], 0)
    return block


def vertical(visc_ref, friction, outside, up_ref, down_ref):
    levels = visc_ref.shape[0] - FIELDS
    half = 0.5 * vert_coupling
    inside = 1.0 - outside

    def eliminate(k, carry):
        low, high = carry
        up_here = visc_ref[k] + outside
        up_next = visc_ref[k + 1] + outside
        link = half * (up_here + up_next)
        ratio = link / (link + low)
        up_ref[k] = ratio
        low = sink_rate * up_next + ratio * low
        m = levels - 2 - k
        down_here = visc_ref[m + 1] + outside
        down_next = visc_ref[m] + outside
        link = half * (down_here + down_next)
        ratio = link / (link + high)
        down_ref[m + 1] = ratio
        high = sink_rate * down_next + ratio * high
        return low, high

    low = sink_rate * (visc_ref[0] + outside) + bed_drag * friction
    high = sink_rate * (visc_ref[levels - 1] + outside)
    low, high = lax.fori_loop(0, levels - 1, eliminate, (low, high))
    top = inside / low
    bed = inside / (high + bed_drag * friction)
    up_ref[levels - 1] = top
    down_ref[0] = bed

    def substitute(k, carry):
        top, bed = carry
        m = levels - 2 - k
        top = up_ref[m] * top
        up_ref[m] = top
        bed = down_ref[k + 1] * bed
        down_ref[k + 1] = bed
        return top, bed

    top, bed = lax.fori_loop(0, levels - 1, substitute, (top, bed))
    return top


def couplings(visc_ref, up_ref, down_ref):
    levels = visc_ref.shape[0] - FIELDS
    shape = visc_ref.shape[1:]
    result = {}
    for step_x in (-1, 0, 1):
        steps_y = (-1, 1) if step_x == 0 else (-1, 0, 1)

        def layer(k, carry, step_x=step_x, steps_y=steps_y):
            sums = carry
            below = jnp.maximum(k - 1, 0)
            above = jnp.minimum(k + 1, levels - 1)
            has_below = jnp.where(k > 0, 1.0, 0.0)
            has_above = jnp.where(k < levels - 1, 1.0, 0.0)
            here = down_ref[k]
            lower = down_ref[below] * has_below
            upper = down_ref[above] * has_above
            sides = lower + upper
            v_here = here * visc_ref[k]
            v_sides = lower * visc_ref[below] + upper * visc_ref[above]
            reach = {}
            for count in (1, 2):
                near = offset_weight * 0.5 / count
                far = offset_weight * 0.5 / (count + 1)
                reach[count] = (near * here + far * sides, near * v_here + far * v_sides)
            top = up_ref[k]
            v_top = moved(top * visc_ref[k], step_x, 0)
            top = moved(top, step_x, 0)
            out = []
            for total, step_y in zip(sums, steps_y):
                plain, heavy = reach[abs(step_x) + abs(step_y)]
                out.append(
                    total + moved(v_top, 0, step_y) * plain + moved(top, 0, step_y) * heavy
                )
            return tuple(out)

        zero = jnp.zeros(shape, jnp.float32)
        sums = lax.fori_loop(0, levels, layer, (zero,) * len(steps_y))
        for step_y, total in zip(steps_y, sums):
            result[step_x, step_y] = total
    return result


def spread(weights, centre, one, two):
    plus = (one + cross_share * two, two + cross_share * one)
    minus = (one - cross_share * two, two - cross_share * one)
    out = [centre * one, centre * two]
    for step_y in (-1, 0, 1):
        side = [moved(x, 0, step_y) for x in (one, two)]
        if step_y:
            pairs = {
                step_y: [moved(x, 0, step_y) for x in plus],
                -step_y: [moved(x, 0, step_y) for x in minus],
            }
            for c in (0, 1):
                out[c] = out[c] + weights[0, step_y] * side[c]
        for step_x in (-1, 1):
            fields = pairs[step_x] if step_y else side
            for c in (0, 1):
                out[c] = out[c] + weights[step_x, step_y] * moved(fields[c], step_x, 0)
    return out


def column_kernel(wide_ref, own_ref, sums_ref, up_ref, down_ref):
    levels = wide_ref.shape[0] - FIELDS
    rows, cols = own_ref.shape[1:]
    friction = wide_ref[levels]
    source = (wide_ref[levels + 1], wide_ref[levels + 2])
    obs = wide_ref[levels + 3]
    inverse_diag = wide_ref[levels + 4]
    gradient = wide_ref[levels + 5]
    warm_start = wide_ref[levels + 6]
    outside = jnp.where(wide_ref[0] > 0.0, 0.0, 1.0)
    through = vertical(wide_ref, friction, outside, up_ref, down_ref)
    back = couplings(wide_ref, up_ref, down_ref)
    forth = {(dx, dy): moved(back[-dx, -dy], dx, dy) for dx, dy in back}

    def hessian(q):
        surface = spread(forth, through, source[0] * q, source[1] * q)
        basal = spread(back, through, obs * surface[0], obs * surface[1])
        beside = moved(q, 1, 0) + moved(q, -1, 0) + moved(q, 0, 1) + moved(q, 0, -1)
        smooth = reg_gamma * (q + reg_smooth * (4.0 * q - beside))
        return source[0] * basal[0] + source[1] * basal[1] + smooth

    residual = gradient - hessian(warm_start)
    direction = inverse_diag * residual
    image = hessian(direction)
    second = inverse_diag * image
    second_image = hessian(second)

    def own(field):
        return field[HALO : HALO + rows, HALO : HALO + cols]

    kept = [own(x) for x in (residual, direction, image, second, second_image)]
    for index, field in enumerate(kept):
        own_ref[index] = field
    residual, direction, image, second, second_image = kept
    parts = (residual * direction, direction * image, second * image, second * second_image)
    for index, part in enumerate(parts):
        sums_ref[index : index + 1] = jnp.sum(part, axis=0, keepdims=True)


def exchanged(block, axis, dim, width):
    count = lax.axis_size(axis)
    forward = [(i, i + 1) for i in range(count - 1)]
    backward = [(target, source) for source, target in forward]
    low = lax.ppermute(
        lax.slice_in_dim(block, block.shape[dim] - width, None, axis=dim), axis, forward
    )
    high = lax.ppermute(lax.slice_in_dim(block, 0, width, axis=dim), axis, backward)
    return jnp.concatenate([low, block, high], axis=dim)


def summed(values):
    for axis in ("gx", "gy"):
        count = lax.axis_size(axis)
        step = 1
        while step < count:
            pairs = [(i, i ^ step) for i in range(count)]
            values = values + lax.ppermute(values, axis, pairs)
            step *= 2
    return values


def on_device(
    gradient, warm_start, viscosity, friction_coef, slide_dir, obs_weight, ice_mask, grounded
):
    levels, rows, cols = viscosity.shape
    ice_float = ice_mask.astype(jnp.float32)
    ground_float = grounded.astype(jnp.float32)
    friction = ground_float * friction_coef
    source = (ice_float * ground_float * friction_coef)[None] * slide_dir
    obs = ice_float * obs_weight
    inverse_diag = 1.0 / (
        reg_gamma * (1.0 + 4.0 * reg_smooth)
        + diag_scale * ice_float * ground_float * friction_coef * friction_coef
    )
    columns = jnp.stack(
        [friction, source[0], source[1], obs, inverse_diag, gradient, warm_start]
    )
    stacked = jnp.concatenate([viscosity, columns], axis=0)
    wide = exchanged(stacked, "gy", 2, HALO)
    wide = exchanged(wide, "gx", 1, HALO)
    span_x = round_up(rows + 2 * HALO, 8)
    span_y = round_up(cols + 2 * HALO, 128)
    wide = jnp.pad(
        wide, ((0, 0), (0, span_x - rows - 2 * HALO), (0, span_y - cols - 2 * HALO))
    )
    own, sums = pl.pallas_call(
        column_kernel,
        out_shape=(
            jax.ShapeDtypeStruct((5, rows, cols), jnp.float32),
            jax.ShapeDtypeStruct((4, cols), jnp.float32),
        ),
        scratch_shapes=[pltpu.VMEM((levels, span_x, span_y), jnp.float32)] * 2,
        name="columns",
    )(wide)
    residual, direction, image, second, second_image = own
    norm_now, curve, cross, second_curve = summed(jnp.sum(sums, axis=1))
    first_step = norm_now / curve
    norm_next = first_step * first_step * cross - norm_now
    ratio = norm_next / norm_now
    grow = 1.0 + ratio
    next_curve = (
        grow * grow * curve
        - 2.0 * grow * first_step * cross
        + first_step * first_step * second_curve
    )
    next_step = norm_next / next_curve
    solution = (
        warm_start
        + first_step * direction
        + next_step * (grow * direction - first_step * second)
    )
    residual = (
        residual - first_step * image - next_step * (grow * image - first_step * second_image)
    )
    return (solution, residual)


def solution(mesh):
    return jax.shard_map(
        on_device,
        mesh=mesh,
        in_specs=(
            P("gx", "gy"),
            P("gx", "gy"),
            P(None, "gx", "gy"),
            P("gx", "gy"),
            P(None, "gx", "gy"),
            P("gx", "gy"),
            P("gx", "gy"),
            P("gx", "gy"),
        ),
        out_specs=(P("gx", "gy"), P("gx", "gy")),
        check_vma=False,
    )
```

time: 330 us -> 81 us (0.25)
  blocking collectives: 125 us -> 0 us
  other arithmetic: 112 us -> 8.97 us
  starting transfers between devices: 54.2 us -> 21.4 us
  Pallas kernels: 0 us -> 16.4 us
  local copies, waits for them, and re-layouts: 12.1 us -> 3.19 us
  waiting for transfers between devices: 18.6 us -> 24 us
    psum x3 -> x0, blocking collectives: 125 us -> none  [the longest x2 82.2 us: residual_dot(): return lax.psum(jnp.sum(residual * precond), ('gx', 'gy'))]
    another operation x13 -> x0, other arithmetic: 80.2 us -> none  [the longest x12 80.2 us: couple(): return jnp.stack([along_one, along_two])]
    ppermute x20 -> x9, starting transfers between devices: 54.2 us -> 21.4 us  [the longest x5 12.9 us: summed(): values = values + lax.ppermute(values, axis, pairs)]
    pallas_call x0 -> x1, Pallas kernels: none -> 16.4 us  [on_device(): pl.pallas_call(column_kernel, out_shape=(jax.ShapeDtypeStruct((5, rows, c...]
    reduce_sum x12 -> x1, other arithmetic: 16.1 us -> 0.81 us  [on_device(): norm_now, curve, cross, second_curve = summed(jnp.sum(sums, axis=1))]
    mul x32 -> x0, other arithmetic: 7.7 us -> none  [the longest x3 2.58 us: hessian(): first_state = bottom_wide[None] * spread[:, None]]
    ppermute x20 -> x9, waiting for transfers between devices: 18.6 us -> 24 us  [the longest x2 8.76 us: exchanged(): lax.ppermute(lax.slice_in_dim(block, 0, width, axis=dim), axis, backward)]
    unnamed x145 -> x4, local copies, waits for them, and re-layouts: 6.44 us -> 1.67 us
  transfers between devices with their start and end apart: 20 -> 9, of which waited for: 6 -> 8; matrix products, arithmetic and copies ran while one was open for 2% -> 0% of each run, Pallas kernels for 0% -> 0%
where the time goes in v1:
time: 81 us; the launch traced here: 79.9 us
  waiting for transfers between devices  24 us (30%)
  starting transfers between devices  21.4 us (26%)
  Pallas kernels  16.4 us (20%)
  other arithmetic  8.97 us (11%)
  between operations  5.93 us (7%)
  local copies, waits for them, and re-layouts  3.19 us (4%)
    pallas_call x1, Pallas kernels, on_device(): pl.pallas_call(column_kernel, out_shape=(jax.ShapeDtypeStruct((5, rows, c...  16.4 us
    ppermute x5, starting transfers between devices, summed(): values = values + lax.ppermute(values, axis, pairs)  12.9 us
    ppermute x2, waiting for transfers between devices, exchanged(): lax.ppermute(lax.slice_in_dim(block, 0, width, axis=dim), axis, backward)  8.76 us
    ppermute x5, waiting for transfers between devices, summed(): values = values + lax.ppermute(values, axis, pairs)  8.09 us
    ppermute x2, waiting for transfers between devices, exchanged(): lax.ppermute(lax.slice_in_dim(block, block.shape[dim] - width, None, axis...  7.16 us
    ppermute x2, starting transfers between devices, exchanged(): lax.ppermute(lax.slice_in_dim(block, block.shape[dim] - width, None, axis...  5.92 us
    unnamed x4, other arithmetic  2.89 us
    ppermute x2, starting transfers between devices, exchanged(): lax.ppermute(lax.slice_in_dim(block, 0, width, axis=dim), axis, backward)  2.58 us
  transfers between devices with their start and end apart: 9, of which 8 were waited for; matrix products, arithmetic and copies ran while one was open for 0% of the time, Pallas kernels for 0%

profile of v1, /device:TPU:0, one launch (start us, length us, event | category | flops | bytes accessed | tf_op | source)
XLA Modules:
  0.0 79.9 jit_solution(8171741858738112081)
XLA Ops:
  0.6 1.0 %constant_dynamic-update-slice_fusion.6 = f32[39,8,256]{2,1,0:T(8,128)S(1)} fusion(f32[32,8,256]{2,1,0:T(8,128)} %param.10), kind=kLoop, calls=%fused_computation.20 | loop fusion | bytes 524288
  1.6 0.7 multiply_multiply_fusion.1
  4.5 0.7 constant_dynamic-update-slice_fusion.2
  6.7 2.4 %collective-permute-start = (f32[39,8,6]{2,1,0:T(8,128)S(1)}, f32[39,8,6]{2,1,0:T(8,128)S(1)}, u32[]{:S(2)}, u32[]{:S(2)}) collective-permute-start(f32[39,8,6]{2,1,0:T(8,128)S(1)} %get-tuple-element.8), channel_id=1, source_target_pairs={{0,1},{1,2},{2,3},{3,4},{4,5},{5,6},{6,7},{8,9},{9,10},{10,11},{11... | collective-permute-start | bytes 22472 | tf_op jit(solution)/shard_map/ppermute | solution.py:181
  9.2 1.3 %collective-permute-start.1 = (f32[39,8,6]{2,1,0:T(8,128)S(1)}, f32[39,8,6]{2,1,0:T(8,128)S(1)}, u32[]{:S(2)}, u32[]{:S(2)}) collective-permute-start(f32[39,8,6]{2,1,0:T(8,128)S(1)} %get-tuple-element.9), channel_id=1, source_target_pairs={{1,0},{2,1},{3,2},{4,3},{5,4},{6,5},{7,6},{9,8},{10,9},{11,10},{12... | collective-permute-start | bytes 22472 | tf_op jit(solution)/shard_map/ppermute | solution.py:184
  10.5 4.1 %collective-permute-done.1 = f32[39,8,6]{2,1,0:T(8,128)S(1)} collective-permute-done((f32[39,8,6]{2,1,0:T(8,128)S(1)}, f32[39,8,6]{2,1,0:T(8,128)S(1)}, u32[]{:S(2)}, u32[]{:S(2)}) %collective-permute-start.1) | collective-permute-done | bytes 7520 | tf_op jit(solution)/shard_map/ppermute | solution.py:184
  14.8 3.5 %collective-permute-start.2 = (f32[39,6,268]{2,1,0:T(8,128)S(1)}, f32[39,6,268]{2,1,0:T(8,128)S(1)}, u32[]{:S(2)}, u32[]{:S(2)}) collective-permute-start(f32[39,6,268]{2,1,0:T(8,128)S(1)} %get-tuple-element.6), channel_id=1, source_target_pairs={{0,8},{8,16},{16,24},{1,9},{9,17},{17,25},{2,10},{10,18},{18,26},{... | collective-permute-start | bytes 752552 | tf_op jit(solution)/shard_map/ppermute | solution.py:181
  18.4 1.3 %collective-permute-start.3 = (f32[39,6,268]{2,1,0:T(8,128)S(1)}, f32[39,6,268]{2,1,0:T(8,128)S(1)}, u32[]{:S(2)}, u32[]{:S(2)}) collective-permute-start(f32[39,6,268]{2,1,0:T(8,128)S(1)} %get-tuple-element.7), channel_id=1, source_target_pairs={{8,0},{16,8},{24,16},{9,1},{17,9},{25,17},{10,2},{18,10},{26,18},{... | collective-permute-start | bytes 752552 | tf_op jit(solution)/shard_map/ppermute | solution.py:184
  19.7 7.2 %collective-permute-done.2 = f32[39,6,268]{2,1,0:T(8,128)S(1)} collective-permute-done((f32[39,6,268]{2,1,0:T(8,128)S(1)}, f32[39,6,268]{2,1,0:T(8,128)S(1)}, u32[]{:S(2)}, u32[]{:S(2)}) %collective-permute-start.2) | collective-permute-done | bytes 250880 | tf_op jit(solution)/shard_map/ppermute | solution.py:181
  26.8 4.7 %collective-permute-done.3 = f32[39,6,268]{2,1,0:T(8,128)S(1)} collective-permute-done((f32[39,6,268]{2,1,0:T(8,128)S(1)}, f32[39,6,268]{2,1,0:T(8,128)S(1)}, u32[]{:S(2)}, u32[]{:S(2)}) %collective-permute-start.3) | collective-permute-done | bytes 250880 | tf_op jit(solution)/shard_map/ppermute | solution.py:184
  31.5 1.6 %select_maximum_fusion.wide_ref = f32[39,24,384]{2,1,0:T(8,128)} fusion(f32[39,6,268]{2,1,0:T(8,128)S(1)} %collective-permute-done.3, f32[39,6,268]{2,1,0:T(8,128)S(1)} %collective-permute-done.2, f32[39,8,6]{2,1,0:T(8,128)S(1)} %collective-permute-done.1, f32[39,8,256]{2,1,0:T(8,128)S(1)} %constant_dynamic-update-slice_fusion, ...), kind=kLoop, calls=%fused_computation | loop fusion | flops 6110208 | bytes 2273856 | tf_op jit(solution)/shard_map/concatenate | solution.py:185
  33.1 16.4 %columns.1 = (f32[5,8,256]{2,1,0:T(8,128)}, f32[4,256]{1,0:T(4,128)}) custom-call(f32[39,24,384]{2,1,0:T(8,128)} %select_maximum_fusion.wide_ref), custom_call_target="tpu_custom_call" | custom-call | tf_op jit(solution)/shard_map/columns/pallas_call | solution.py:223
  49.5 0.8 %reduce_sum.9 = f32[4]{0:T(128)S(1)} reduce(f32[4,256]{1,0:T(4,128)} %get-tuple-element.4, f32[]{:T(128)} %constant.2.clone.1), dimensions={1}, to_apply=%region_0.1 | reduce | flops 1020 | bytes 4116 | tf_op jit(solution)/shard_map/reduce_sum | solution.py:233
  50.4 1.6 %collective-permute-start.4 = (f32[4]{0:T(128)S(1)}, f32[4]{0:T(128)S(1)}, u32[]{:S(2)}, u32[]{:S(2)}) collective-permute-start(f32[4]{0:T(128)S(1)} %reduce_sum.9), channel_id=1, source_target_pairs={{0,8},{8,0},{16,24},{24,16},{1,9},{9,1},{17,25},{25,17},{2,10},{10... | collective-permute-start | bytes 56 | tf_op jit(solution)/shard_map/ppermute | solution.py:194
  52.0 2.0 %collective-permute-done.4 = f32[4]{0:T(128)S(1)} collective-permute-done((f32[4]{0:T(128)S(1)}, f32[4]{0:T(128)S(1)}, u32[]{:S(2)}, u32[]{:S(2)}) %collective-permute-start.4) | collective-permute-done | bytes 48 | tf_op jit(solution)/shard_map/ppermute | solution.py:194
  54.0 2.6 %collective-permute-start.5 = (f32[4]{0:T(128)S(1)}, f32[4]{0:T(128)S(1)}, u32[]{:S(2)}, u32[]{:S(2)}) collective-permute-start(f32[4]{0:T(128)S(1)} %add.37), channel_id=1, source_target_pairs={{0,16},{8,24},{16,0},{24,8},{1,17},{9,25},{17,1},{25,9},{2,18},{10... | collective-permute-start | bytes 56 | tf_op jit(solution)/shard_map/ppermute | solution.py:194
  56.5 1.9 %collective-permute-done.5 = f32[4]{0:T(128)S(1)} collective-permute-done((f32[4]{0:T(128)S(1)}, f32[4]{0:T(128)S(1)}, u32[]{:S(2)}, u32[]{:S(2)}) %collective-permute-start.5) | collective-permute-done | bytes 48 | tf_op jit(solution)/shard_map/ppermute | solution.py:194
  58.5 1.1 %collective-permute-done.6 = f32[4]{0:T(128)S(1)} collective-permute-done((f32[4]{0:T(128)S(1)}, f32[4]{0:T(128)S(1)}, u32[]{:S(2)}, u32[]{:S(2)}) %collective-permute-start.6) | collective-permute-done | bytes 48 | tf_op jit(solution)/shard_map/ppermute | solution.py:194
  59.6 4.7 %collective-permute-start.7 = (f32[4]{0:T(128)S(1)}, f32[4]{0:T(128)S(1)}, u32[]{:S(2)}, u32[]{:S(2)}) collective-permute-start(f32[4]{0:T(128)S(1)} %add.39), channel_id=1, source_target_pairs={{0,2},{1,3},{2,0},{3,1},{4,6},{5,7},{6,4},{7,5},{8,10},{9,11},{10,... | collective-permute-start | bytes 56 | tf_op jit(solution)/shard_map/ppermute | solution.py:194
  64.3 1.5 %collective-permute-done.7 = f32[4]{0:T(128)S(1)} collective-permute-done((f32[4]{0:T(128)S(1)}, f32[4]{0:T(128)S(1)}, u32[]{:S(2)}, u32[]{:S(2)}) %collective-permute-start.7) | collective-permute-done | bytes 48 | tf_op jit(solution)/shard_map/ppermute | solution.py:194
  65.8 4.0 %collective-permute-start.8 = (f32[4]{0:T(128)S(1)}, f32[4]{0:T(128)S(1)}, u32[]{:S(2)}, u32[]{:S(2)}) collective-permute-start(f32[4]{0:T(128)S(1)} %add.40), channel_id=1, source_target_pairs={{0,4},{1,5},{2,6},{3,7},{4,0},{5,1},{6,2},{7,3},{8,12},{9,13},{10,... | collective-permute-start | bytes 56 | tf_op jit(solution)/shard_map/ppermute | solution.py:194
  69.8 1.5 %collective-permute-done.8 = f32[4]{0:T(128)S(1)} collective-permute-done((f32[4]{0:T(128)S(1)}, f32[4]{0:T(128)S(1)}, u32[]{:S(2)}, u32[]{:S(2)}) %collective-permute-start.8) | collective-permute-done | bytes 48 | tf_op jit(solution)/shard_map/ppermute | solution.py:194
  77.3 1.3 %subtract_bitcast_fusion = f32[8,256]{1,0:T(8,128)} fusion(f32[5,8,256]{2,1,0:T(8,128)} %get-tuple-element.5, f32[]{:T(128)S(6)} %add.43, f32[]{:T(128)S(6)} %div.19, f32[]{:T(128)S(6)} %div.17), kind=kLoop, calls=%fused_computation.27 | loop fusion | flops 14336 | bytes 32780 | tf_op jit(solution)/shard_map/sub | solution.py:250
  78.6 1.3 %bitcast_add_fusion = f32[8,256]{1,0:T(8,128)} fusion(f32[8,256]{1,0:T(8,128)S(1)} %copy-done, f32[5,8,256]{2,1,0:T(8,128)} %get-tuple-element.5, f32[]{:T(128)S(6)} %add.43, f32[]{:T(128)S(6)} %div.19, f32[]{:T(128)S(6)} %div.17), kind=kLoop, calls=%fused_computation.25 | loop fusion | flops 14336 | bytes 32780 | tf_op jit(solution)/shard_map/add | solution.py:245
  (18 shorter events, 4.7 us)
Async XLA Ops:
  6.7 3.7 %collective-permute-start = (f32[39,8,6]{2,1,0:T(8,128)S(1)}, f32[39,8,6]{2,1,0:T(8,128)S(1)}, u32[]{:S(2)}, u32[]{:S(2)}) collective-permute-start(f32[39,8,6]{2,1,0:T(8,128)S(1)} %get-tuple-element.8), channel_id=1, source_target_pairs={{0,1},{1,2},{2,3},{3,4},{4,5},{5,6},{6,7},{8,9},{9,10},{10,11},{11... | collective-permute-start | bytes 22472 | tf_op jit(solution)/shard_map/ppermute | solution.py:181
  9.2 5.4 %collective-permute-start.1 = (f32[39,8,6]{2,1,0:T(8,128)S(1)}, f32[39,8,6]{2,1,0:T(8,128)S(1)}, u32[]{:S(2)}, u32[]{:S(2)}) collective-permute-start(f32[39,8,6]{2,1,0:T(8,128)S(1)} %get-tuple-element.9), channel_id=1, source_target_pairs={{1,0},{2,1},{3,2},{4,3},{5,4},{6,5},{7,6},{9,8},{10,9},{11,10},{12... | collective-permute-start | bytes 22472 | tf_op jit(solution)/shard_map/ppermute | solution.py:184
  14.8 12.0 %collective-permute-start.2 = (f32[39,6,268]{2,1,0:T(8,128)S(1)}, f32[39,6,268]{2,1,0:T(8,128)S(1)}, u32[]{:S(2)}, u32[]{:S(2)}) collective-permute-start(f32[39,6,268]{2,1,0:T(8,128)S(1)} %get-tuple-element.6), channel_id=1, source_target_pairs={{0,8},{8,16},{16,24},{1,9},{9,17},{17,25},{2,10},{10,18},{18,26},{... | collective-permute-start | bytes 752552 | tf_op jit(solution)/shard_map/ppermute | solution.py:181
  18.4 13.2 %collective-permute-start.3 = (f32[39,6,268]{2,1,0:T(8,128)S(1)}, f32[39,6,268]{2,1,0:T(8,128)S(1)}, u32[]{:S(2)}, u32[]{:S(2)}) collective-permute-start(f32[39,6,268]{2,1,0:T(8,128)S(1)} %get-tuple-element.7), channel_id=1, source_target_pairs={{8,0},{16,8},{24,16},{9,1},{17,9},{25,17},{10,2},{18,10},{26,18},{... | collective-permute-start | bytes 752552 | tf_op jit(solution)/shard_map/ppermute | solution.py:184
  33.1 45.5 %copy-start = (f32[8,256]{1,0:T(8,128)S(1)}, f32[8,256]{1,0:T(8,128)}, u32[]{:S(2)}) copy-start(f32[8,256]{1,0:T(8,128)} %param.9) | copy-start | bytes 24580
  50.4 3.6 %collective-permute-start.4 = (f32[4]{0:T(128)S(1)}, f32[4]{0:T(128)S(1)}, u32[]{:S(2)}, u32[]{:S(2)}) collective-permute-start(f32[4]{0:T(128)S(1)} %reduce_sum.9), channel_id=1, source_target_pairs={{0,8},{8,0},{16,24},{24,16},{1,9},{9,1},{17,25},{25,17},{2,10},{10... | collective-permute-start | bytes 56 | tf_op jit(solution)/shard_map/ppermute | solution.py:194
  54.0 4.5 %collective-permute-start.5 = (f32[4]{0:T(128)S(1)}, f32[4]{0:T(128)S(1)}, u32[]{:S(2)}, u32[]{:S(2)}) collective-permute-start(f32[4]{0:T(128)S(1)} %add.37), channel_id=1, source_target_pairs={{0,16},{8,24},{16,0},{24,8},{1,17},{9,25},{17,1},{25,9},{2,18},{10... | collective-permute-start | bytes 56 | tf_op jit(solution)/shard_map/ppermute | solution.py:194
  58.5 1.2 %collective-permute-start.6 = (f32[4]{0:T(128)S(1)}, f32[4]{0:T(128)S(1)}, u32[]{:S(2)}, u32[]{:S(2)}) collective-permute-start(f32[4]{0:T(128)S(1)} %add.38), channel_id=1, source_target_pairs={{0,1},{1,0},{2,3},{3,2},{4,5},{5,4},{6,7},{7,6},{8,9},{9,8},{10,11... | collective-permute-start | bytes 56 | tf_op jit(solution)/shard_map/ppermute | solution.py:194
  59.6 6.2 %collective-permute-start.7 = (f32[4]{0:T(128)S(1)}, f32[4]{0:T(128)S(1)}, u32[]{:S(2)}, u32[]{:S(2)}) collective-permute-start(f32[4]{0:T(128)S(1)} %add.39), channel_id=1, source_target_pairs={{0,2},{1,3},{2,0},{3,1},{4,6},{5,7},{6,4},{7,5},{8,10},{9,11},{10,... | collective-permute-start | bytes 56 | tf_op jit(solution)/shard_map/ppermute | solution.py:194
  65.8 5.5 %collective-permute-start.8 = (f32[4]{0:T(128)S(1)}, f32[4]{0:T(128)S(1)}, u32[]{:S(2)}, u32[]{:S(2)}) collective-permute-start(f32[4]{0:T(128)S(1)} %add.40), channel_id=1, source_target_pairs={{0,4},{1,5},{2,6},{3,7},{4,0},{5,1},{6,2},{7,3},{8,12},{9,13},{10,... | collective-permute-start | bytes 56 | tf_op jit(solution)/shard_map/ppermute | solution.py:194

commit v2 on v1

v2 whole, which is shorter than its diff:
```python
import jax
import jax.numpy as jnp
from jax import lax
from jax.experimental import pallas as pl
from jax.experimental.pallas import tpu as pltpu
from jax.sharding import PartitionSpec as P

vert_coupling = 128.0
sink_rate = 0.0625
bed_drag = 0.5
offset_weight = 0.0019
cross_share = 0.5
reg_gamma = 0.02
reg_smooth = 1.0
diag_scale = 0.003

HALO = 6
FIELDS = 7
LANES = 128
SLOTS = LANES // HALO
UNROLL = 4


def moved(block, step_x, step_y):
    if step_y:
        block = pltpu.roll(block, (-step_y) % block.shape[1], 1)
    if step_x:
        block = pltpu.roll(block, (-step_x) % block.shape[0], 0)
    return block


def turned(block, amount):
    amount %= LANES
    return pltpu.roll(block, amount, 1) if amount else block


def field_kernel(gradient, warm_start, friction_coef, slide, obs_weight, ice, grounded, out_ref):
    ice_float = ice[...].astype(jnp.float32)
    ground_float = grounded[...].astype(jnp.float32)
    coef = friction_coef[...]
    source = ice_float * ground_float * coef
    out_ref[0] = ground_float * coef
    out_ref[1] = source * slide[0]
    out_ref[2] = source * slide[1]
    out_ref[3] = ice_float * obs_weight[...]
    out_ref[4] = 1.0 / (
        reg_gamma * (1.0 + 4.0 * reg_smooth)
        + diag_scale * ice_float * ground_float * coef * coef
    )
    out_ref[5] = gradient[...]
    out_ref[6] = warm_start[...]


def pack_kernel(*refs):
    layers, fields = refs[0:3], refs[3:6]
    to_low, to_high = refs[6:8]
    levels, rows, cols = layers[0].shape
    lane = lax.broadcasted_iota(jnp.int32, (rows, LANES), 1)
    for t in range(3):
        for group in range(0, levels + FIELDS, SLOTS):
            first = jnp.zeros((rows, LANES), jnp.float32)
            last = first
            for z in range(group, min(group + SLOTS, levels + FIELDS)):
                ref, index = (layers[t], z) if z < levels else (fields[t], z - levels)
                at = HALO * (z - group)
                here = (lane >= at) & (lane < at + HALO)
                first = jnp.where(here, turned(ref[index, :, :LANES], at), first)
                shift = at - (LANES - HALO)
                last = jnp.where(here, turned(ref[index, :, cols - LANES :], shift), last)
            place = (group // SLOTS) * LANES
            to_low[t * rows : (t + 1) * rows, place : place + LANES] = first
            to_high[t * rows : (t + 1) * rows, place : place + LANES] = last


def assemble(layers, fields, from_low, from_high, wide_ref):
    levels, rows, cols = layers[0].shape
    lane = lax.broadcasted_iota(jnp.int32, (rows, LANES), 1)
    for z in range(levels + FIELDS):
        at = HALO * (z % SLOTS)
        place = (z // SLOTS) * LANES
        for t in range(3):
            ref, index = (layers[t], z) if z < levels else (fields[t], z - levels)
            band = slice(t * rows, (t + 1) * rows)
            wide_ref[z, band, :cols] = ref[index]
            high = turned(from_high[band, place : place + LANES], -at)
            low = turned(from_low[band, place : place + LANES], LANES - HALO - at)
            edge = jnp.where(lane < HALO, high, jnp.where(lane >= LANES - HALO, low, 0.0))
            wide_ref[z, band, cols:] = edge


def vertical(wide_ref, tops, heavy_tops, bed_ref, heavy_bed):
    levels = wide_ref.shape[0] - FIELDS
    half = 0.5 * vert_coupling
    friction = bed_drag * wide_ref[levels]
    inside = jnp.where(wide_ref[0] > 0.0, 1.0, 0.0)
    outside = 1.0 - inside
    up_ref = tops[1]

    def eliminate(k, carry):
        low, high, up_here, down_here = carry
        up_next = wide_ref[k + 1] + outside
        link = half * (up_here + up_next)
        ratio = link / (link + low)
        up_ref[k] = ratio
        low = sink_rate * up_next + ratio * low
        m = levels - 2 - k
        down_next = wide_ref[m] + outside
        link = half * (down_here + down_next)
        ratio = link / (link + high)
        bed_ref[m + 2] = ratio
        high = sink_rate * down_next + ratio * high
        return low, high, up_next, down_next

    up_here = wide_ref[0] + outside
    down_here = wide_ref[levels - 1] + outside
    low = sink_rate * up_here + friction
    high = sink_rate * down_here
    low, high, _, _ = lax.fori_loop(0, levels - 1, eliminate, (low, high, up_here, down_here))

    def keep(k, top, m, bed):
        heavy = top * wide_ref[k]
        for index, step in enumerate((-1, 0, 1)):
            tops[index][k] = moved(top, step, 0)
            heavy_tops[index][k] = moved(heavy, step, 0)
        bed_ref[m + 1] = bed
        heavy_bed[m + 1] = bed * wide_ref[m]

    def substitute(k, carry):
        top, bed = carry
        m = levels - 2 - k
        top = up_ref[m] * top
        bed = bed_ref[k + 2] * bed
        keep(m, top, k + 1, bed)
        return top, bed

    top = inside / low
    bed = inside / (high + friction)
    keep(levels - 1, top, 0, bed)
    zero = jnp.zeros(bed.shape, jnp.float32)
    for ref in (bed_ref, heavy_bed):
        ref[0] = zero
        ref[levels + 1] = zero
    top, bed = lax.fori_loop(0, levels - 1, substitute, (top, bed))
    return top


def couplings(levels, rows, tops, heavy_tops, bed_ref, heavy_bed):
    span_x, span_y = bed_ref.shape[1:]
    offsets = [(dx, dy) for dx in (-1, 0, 1) for dy in (-1, 0, 1) if dx or dy]
    unroll = UNROLL if levels % UNROLL == 0 else 1
    bands = []
    for start in range(0, span_x, rows):
        band = slice(start, start + rows)

        def layer(k, sums):
            reach = {}
            here, sides = bed_ref[k + 1, band], bed_ref[k, band] + bed_ref[k + 2, band]
            v_here = heavy_bed[k + 1, band]
            v_sides = heavy_bed[k, band] + heavy_bed[k + 2, band]
            for count in (1, 2):
                near = offset_weight * 0.5 / count
                far = offset_weight * 0.5 / (count + 1)
                plain, heavy = near * here + far * sides, near * v_here + far * v_sides
                for step_y in (-1, 0, 1):
                    if count == 1 or step_y:
                        reach[count, step_y] = (moved(plain, 0, -step_y), moved(heavy, 0, -step_y))
            out = []
            for (step_x, step_y), total in zip(offsets, sums):
                plain, heavy = reach[abs(step_x) + abs(step_y), step_y]
                top, v_top = tops[step_x + 1][k, band], heavy_tops[step_x + 1][k, band]
                out.append(total + (v_top * plain + top * heavy))
            return tuple(out)

        def layers(block, sums):
            for i in range(unroll):
                sums = layer(block * unroll + i, sums)
            return sums

        zero = jnp.zeros((rows, span_y), jnp.float32)
        bands.append(lax.fori_loop(0, levels // unroll, layers, (zero,) * len(offsets)))
    return {
        (dx, dy): moved(jnp.concatenate([band[i] for band in bands], axis=0), 0, dy)
        for i, (dx, dy) in enumerate(offsets)
    }


def spread(weights, centre, one, two):
    plus = (one + cross_share * two, two + cross_share * one)
    minus = (one - cross_share * two, two - cross_share * one)
    out = [centre * one, centre * two]
    for step_y in (-1, 0, 1):
        side = [moved(x, 0, step_y) for x in (one, two)]
        if step_y:
            pairs = {
                step_y: [moved(x, 0, step_y) for x in plus],
                -step_y: [moved(x, 0, step_y) for x in minus],
            }
            for c in (0, 1):
                out[c] = out[c] + weights[0, step_y] * side[c]
        for step_x in (-1, 1):
            fields = pairs[step_x] if step_y else side
            for c in (0, 1):
                out[c] = out[c] + weights[step_x, step_y] * moved(fields[c], step_x, 0)
    return out


def column_kernel(*refs):
    layers, fields, (from_low, from_high) = refs[0:3], refs[3:6], refs[6:8]
    own_ref, sums_ref, wide_ref = refs[8:11]
    tops, heavy_tops, (bed_ref, heavy_bed) = refs[11:14], refs[14:17], refs[17:19]
    levels, rows, cols = layers[0].shape
    assemble(layers, fields, from_low, from_high, wide_ref)
    through = vertical(wide_ref, tops, heavy_tops, bed_ref, heavy_bed)
    back = couplings(levels, rows, tops, heavy_tops, bed_ref, heavy_bed)
    forth = {(dx, dy): moved(back[-dx, -dy], dx, dy) for dx, dy in back}
    source = (wide_ref[levels + 1], wide_ref[levels + 2])
    obs, inverse_diag = wide_ref[levels + 3], wide_ref[levels + 4]
    gradient, warm_start = wide_ref[levels + 5], wide_ref[levels + 6]

    def hessian(q):
        surface = spread(forth, through, source[0] * q, source[1] * q)
        basal = spread(back, through, obs * surface[0], obs * surface[1])
        beside = moved(q, 1, 0) + moved(q, -1, 0) + moved(q, 0, 1) + moved(q, 0, -1)
        smooth = reg_gamma * (q + reg_smooth * (4.0 * q - beside))
        return source[0] * basal[0] + source[1] * basal[1] + smooth

    residual = gradient - hessian(warm_start)
    direction = inverse_diag * residual
    image = hessian(direction)
    second = inverse_diag * image
    second_image = hessian(second)
    kept = [x[:rows, :cols] for x in (residual, direction, image, second, second_image)]
    for index, field in enumerate(kept):
        own_ref[index] = field
    residual, direction, image, second, second_image = kept
    parts = (residual * direction, direction * image, second * image, second * second_image)
    rows_of_sums = []
    for part in parts:
        total = jnp.sum(part, axis=0, keepdims=True)
        rows_of_sums.append(sum(total[:, i : i + LANES] for i in range(0, cols, LANES)))
    sums = jnp.concatenate(rows_of_sums, axis=0)
    for device in range(sums_ref.shape[0]):
        sums_ref[device] = sums


def finish_kernel(sums_ref, own_ref, warm_start, solution_ref, residual_ref):
    sums = jnp.sum(jnp.sum(sums_ref[...], axis=0), axis=1, keepdims=True)
    norm_now, curve, cross, second_curve = (sums[i : i + 1] for i in range(4))
    residual, direction, image, second, second_image = (own_ref[i] for i in range(5))
    first_step = norm_now / curve
    norm_next = first_step * first_step * cross - norm_now
    grow = 1.0 + norm_next / norm_now
    next_curve = (
        grow * grow * curve
        - 2.0 * grow * first_step * cross
        + first_step * first_step * second_curve
    )
    next_step = norm_next / next_curve
    solution_ref[...] = (
        warm_start[...]
        + first_step * direction
        + next_step * (grow * direction - first_step * second)
    )
    residual_ref[...] = (
        residual - first_step * image - next_step * (grow * image - first_step * second_image)
    )


def neighbours(axis):
    forward = [(i, i + 1) for i in range(lax.axis_size(axis) - 1)]
    return forward, [(target, source) for source, target in forward]


def on_device(
    gradient, warm_start, viscosity, friction_coef, slide_dir, obs_weight, ice_mask, grounded
):
    levels, rows, cols = viscosity.shape
    forward, backward = neighbours("gx")
    layers = (
        viscosity,
        lax.ppermute(viscosity, "gx", backward),
        lax.ppermute(viscosity, "gx", forward),
    )
    own_fields = pl.pallas_call(
        field_kernel,
        out_shape=jax.ShapeDtypeStruct((FIELDS, rows, cols), jnp.float32),
        name="fields",
    )(gradient, warm_start, friction_coef, slide_dir, obs_weight, ice_mask, grounded)
    fields = (
        own_fields,
        lax.ppermute(own_fields, "gx", backward),
        lax.ppermute(own_fields, "gx", forward),
    )
    packed = jax.ShapeDtypeStruct(
        (3 * rows, -(-(levels + FIELDS) // SLOTS) * LANES), jnp.float32
    )
    to_low, to_high = pl.pallas_call(pack_kernel, out_shape=(packed, packed), name="pack")(
        *layers, *fields
    )
    forward, backward = neighbours("gy")
    from_high = lax.ppermute(to_low, "gy", backward)
    from_low = lax.ppermute(to_high, "gy", forward)
    devices = lax.axis_size("gx") * lax.axis_size("gy")
    span = (3 * rows, cols + LANES)
    own, sums = pl.pallas_call(
        column_kernel,
        out_shape=(
            jax.ShapeDtypeStruct((5, rows, cols), jnp.float32),
            jax.ShapeDtypeStruct((devices, 4, LANES), jnp.float32),
        ),
        scratch_shapes=[pltpu.VMEM((levels + FIELDS,) + span, jnp.float32)]
        + [pltpu.VMEM((levels,) + span, jnp.float32)] * 6
        + [pltpu.VMEM((levels + 2,) + span, jnp.float32)] * 2,
        name="columns",
    )(*layers, *fields, from_low, from_high)
    sums = lax.all_to_all(sums, ("gx", "gy"), 0, 0)
    return pl.pallas_call(
        finish_kernel,
        out_shape=(jax.ShapeDtypeStruct((rows, cols), jnp.float32),) * 2,
        name="finish",
    )(sums, own, warm_start)


def solution(mesh):
    return jax.shard_map(
        on_device,
        mesh=mesh,
        in_specs=(
            P("gx", "gy"),
            P("gx", "gy"),
            P(None, "gx", "gy"),
            P("gx", "gy"),
            P(None, "gx", "gy"),
            P("gx", "gy"),
            P("gx", "gy"),
            P("gx", "gy"),
        ),
        out_specs=(P("gx", "gy"), P("gx", "gy")),
        check_vma=False,
    )
```

time: 81 us -> 56 us (0.69)
  waiting for transfers between devices: 24 us -> 8.69 us
  blocking collectives: 0 us -> 14.5 us
  other arithmetic: 8.97 us -> 0 us
  starting transfers between devices: 21.4 us -> 14.7 us
  between operations: 5.93 us -> 0.72 us
  Pallas kernels: 16.4 us -> 15 us
  local copies, waits for them, and re-layouts: 3.19 us -> 2.02 us
    ppermute x9 -> x6, waiting for transfers between devices: 24 us -> 8.69 us  [the longest x1 4.15 us: on_device(): lax.ppermute(own_fields, 'gx', backward)]
    all_to_all x0 -> x1, blocking collectives: none -> 14.5 us  [on_device(): sums = lax.all_to_all(sums, ('gx', 'gy'), 0, 0)]
    ppermute x9 -> x6, starting transfers between devices: 21.4 us -> 14.7 us  [the longest x1 4.97 us: on_device(): lax.ppermute(viscosity, 'gx', forward)]
    pallas_call x1, Pallas kernels: 16.4 us -> 9.89 us  [on_device(): pl.pallas_call(column_kernel, out_shape=(jax.ShapeDtypeStruct((5, rows, c...]
    pallas_call x0 -> x3, Pallas kernels: none -> 5.13 us  [the longest x1 2.06 us: on_device(): pl.pallas_call(pack_kernel, out_shape=(packed, packed), name='pack')]
    unnamed x4 -> x0, other arithmetic: 2.89 us -> none
    concatenate x2 -> x0, other arithmetic: 1.86 us -> none  [exchanged(): return jnp.concatenate([low, block, high], axis=dim)]
    sub x1 -> x0, other arithmetic: 1.34 us -> none  [on_device(): residual - first_step * image]
  transfers between devices with their start and end apart: 9 -> 6, of which waited for: 8 -> 3; matrix products, arithmetic and copies ran while one was open for 0% -> 0% of each run, Pallas kernels for 0% -> 3%
where the time goes in v2:
time: 56 us; the launch traced here: 55.6 us
  Pallas kernels  15 us (27%)
  starting transfers between devices  14.7 us (26%)
  blocking collectives  14.5 us (26%)
  waiting for transfers between devices  8.69 us (16%)
  local copies, waits for them, and re-layouts  2.02 us (4%)
  between operations  0.72 us (1%)
    all_to_all x1, blocking collectives, on_device(): sums = lax.all_to_all(sums, ('gx', 'gy'), 0, 0)  14.5 us
    pallas_call x1, Pallas kernels, on_device(): pl.pallas_call(column_kernel, out_shape=(jax.ShapeDtypeStruct((5, rows, c...  9.89 us
    ppermute x1, starting transfers between devices, on_device(): lax.ppermute(viscosity, 'gx', forward)  4.97 us
    ppermute x1, starting transfers between devices, on_device(): lax.ppermute(own_fields, 'gx', forward)  4.54 us
    ppermute x1, waiting for transfers between devices, on_device(): lax.ppermute(own_fields, 'gx', backward)  4.15 us
    ppermute x1, waiting for transfers between devices, on_device(): from_high = lax.ppermute(to_low, 'gy', backward)  3.7 us
    pallas_call x1, Pallas kernels, on_device(): pl.pallas_call(pack_kernel, out_shape=(packed, packed), name='pack')  2.06 us
    unnamed x12, local copies, waits for them, and re-layouts  2.02 us
  transfers between devices with their start and end apart: 6, of which 3 were waited for; matrix products, arithmetic and copies ran while one was open for 0% of the time, Pallas kernels for 3%

profile of v2, /device:TPU:0, one launch (start us, length us, event | category | flops | bytes accessed | tf_op | source)
XLA Modules:
  0.0 55.6 jit_solution(15698368169305086029)
XLA Ops:
  0.6 5.0 %collective-permute-start.1 = (f32[32,8,256]{2,1,0:T(8,128)}, f32[32,8,256]{2,1,0:T(8,128)S(1)}, u32[]{:S(2)}, u32[]{:S(2)}) collective-permute-start(f32[32,8,256]{2,1,0:T(8,128)} %refs_0_.3), channel_id=1, source_target_pairs={{0,8},{8,16},{16,24},{1,9},{9,17},{17,25},{2,10},{10,18},{18,26},{... | collective-permute-start | bytes 786440 | tf_op jit(solution)/shard_map/ppermute | solution.py:282
  5.6 1.3 %collective-permute-start = (f32[32,8,256]{2,1,0:T(8,128)}, f32[32,8,256]{2,1,0:T(8,128)S(1)}, u32[]{:S(2)}, u32[]{:S(2)}) collective-permute-start(f32[32,8,256]{2,1,0:T(8,128)} %refs_0_.3), channel_id=1, source_target_pairs={{8,0},{16,8},{24,16},{9,1},{17,9},{25,17},{10,2},{18,10},{26,18},{... | collective-permute-start | bytes 786440 | tf_op jit(solution)/shard_map/ppermute | solution.py:281
  6.9 1.4 %fields.1.refs_3_ = f32[7,8,256]{2,1,0:T(8,128)} custom-call(f32[8,256]{1,0:T(8,128)} %gradient.1, f32[8,256]{1,0:T(8,128)} %warm_start.3, f32[8,256]{1,0:T(8,128)} %friction_coef.1, f32[2,8,256]{2,1,0:T(8,128)} %slide.1, f32[8,256]{1,0:T(8,128)} %obs_weight.1, s32[8,256]{1,0:T(8,128)} %ice.1, s32[8,256]{1,0:T(8,128)} %grounded.1), custom_call_target="tpu_custom_call" | custom-call | tf_op jit(solution)/shard_map/fields/pallas_call | solution.py:284
  8.3 4.5 %collective-permute-start.3 = (f32[7,8,256]{2,1,0:T(8,128)}, f32[7,8,256]{2,1,0:T(8,128)S(1)}, u32[]{:S(2)}, u32[]{:S(2)}) collective-permute-start(f32[7,8,256]{2,1,0:T(8,128)} %fields.1.refs_3_), channel_id=1, source_target_pairs={{0,8},{8,16},{16,24},{1,9},{9,17},{17,25},{2,10},{10,18},{18,26},{... | collective-permute-start | bytes 172040 | tf_op jit(solution)/shard_map/ppermute | solution.py:292
  12.9 1.3 %collective-permute-start.2 = (f32[7,8,256]{2,1,0:T(8,128)}, f32[7,8,256]{2,1,0:T(8,128)S(1)}, u32[]{:S(2)}, u32[]{:S(2)}) collective-permute-start(f32[7,8,256]{2,1,0:T(8,128)} %fields.1.refs_3_), channel_id=1, source_target_pairs={{8,0},{16,8},{24,16},{9,1},{17,9},{25,17},{10,2},{18,10},{26,18},{... | collective-permute-start | bytes 172040 | tf_op jit(solution)/shard_map/ppermute | solution.py:291
  14.2 0.8 %collective-permute-done.3.refs_5_ = f32[7,8,256]{2,1,0:T(8,128)S(1)} collective-permute-done((f32[7,8,256]{2,1,0:T(8,128)}, f32[7,8,256]{2,1,0:T(8,128)S(1)}, u32[]{:S(2)}, u32[]{:S(2)}) %collective-permute-start.3) | collective-permute-done | bytes 57376 | tf_op jit(solution)/shard_map/ppermute | solution.py:292
  15.0 4.2 %collective-permute-done.2.refs_4_ = f32[7,8,256]{2,1,0:T(8,128)S(1)} collective-permute-done((f32[7,8,256]{2,1,0:T(8,128)}, f32[7,8,256]{2,1,0:T(8,128)S(1)}, u32[]{:S(2)}, u32[]{:S(2)}) %collective-permute-start.2) | collective-permute-done | bytes 57376 | tf_op jit(solution)/shard_map/ppermute | solution.py:291
  19.2 0.0 collective-permute-done.1.refs_2_
  19.2 0.0 collective-permute-done.refs_1_
  19.2 0.0 copy-done.2
  19.2 0.6 %copy-done.3 = f32[7,8,256]{2,1,0:T(8,128)} copy-done((f32[7,8,256]{2,1,0:T(8,128)}, f32[7,8,256]{2,1,0:T(8,128)S(1)}, u32[]{:S(2)}) %copy-start.3) | copy-done | bytes 57368
  19.8 0.1 copy-done
  19.9 0.7 %copy-done.1 = f32[32,8,256]{2,1,0:T(8,128)} copy-done((f32[32,8,256]{2,1,0:T(8,128)}, f32[32,8,256]{2,1,0:T(8,128)S(1)}, u32[]{:S(2)}) %copy-start.1) | copy-done | bytes 262168
  20.6 2.1 %pack.1 = (f32[24,256]{1,0:T(8,128)}, f32[24,256]{1,0:T(8,128)}) custom-call(f32[32,8,256]{2,1,0:T(8,128)} %refs_0_.3, f32[32,8,256]{2,1,0:T(8,128)} %copy-done.1, f32[32,8,256]{2,1,0:T(8,128)} %copy-done, f32[7,8,256]{2,1,0:T(8,128)} %fields.1.refs_3_, f32[7,8,256]{2,1,0:T(8,128)} %copy-done.3, f32[7,8,256]{2,1,0:T(8,128)} %copy-done.2), custom_call_target="tpu_custom_call" | custom-call | tf_op jit(solution)/shard_map/pack/pallas_call | solution.py:297
  22.6 1.3 %collective-permute-start.4 = (f32[24,256]{1,0:T(8,128)}, f32[24,256]{1,0:T(8,128)S(1)}, u32[]{:S(2)}, u32[]{:S(2)}) collective-permute-start(f32[24,256]{1,0:T(8,128)} %get-tuple-element.6), channel_id=1, source_target_pairs={{0,1},{1,2},{2,3},{3,4},{4,5},{5,6},{6,7},{8,9},{9,10},{10,11},{11... | collective-permute-start | bytes 73736 | tf_op jit(solution)/shard_map/ppermute | solution.py:302
  23.9 1.3 %collective-permute-start.5 = (f32[24,256]{1,0:T(8,128)}, f32[24,256]{1,0:T(8,128)S(1)}, u32[]{:S(2)}, u32[]{:S(2)}) collective-permute-start(f32[24,256]{1,0:T(8,128)} %get-tuple-element.7), channel_id=1, source_target_pairs={{1,0},{2,1},{3,2},{4,3},{5,4},{6,5},{7,6},{9,8},{10,9},{11,10},{12... | collective-permute-start | bytes 73736 | tf_op jit(solution)/shard_map/ppermute | solution.py:301
  25.2 0.0 collective-permute-done.4.refs_6_
  25.2 0.0 copy-start.4
  25.3 3.7 %collective-permute-done.5.refs_7_ = f32[24,256]{1,0:T(8,128)S(1)} collective-permute-done((f32[24,256]{1,0:T(8,128)}, f32[24,256]{1,0:T(8,128)S(1)}, u32[]{:S(2)}, u32[]{:S(2)}) %collective-permute-start.5) | collective-permute-done | bytes 24608 | tf_op jit(solution)/shard_map/ppermute | solution.py:301
  29.0 0.0 copy-done.4
  29.0 0.6 %copy-done.5 = f32[24,256]{1,0:T(8,128)} copy-done((f32[24,256]{1,0:T(8,128)}, f32[24,256]{1,0:T(8,128)S(1)}, u32[]{:S(2)}) %copy-start.5) | copy-done | bytes 24600
  29.6 9.9 %columns.1 = (f32[5,8,256]{2,1,0:T(8,128)}, f32[32,4,128]{2,1,0:T(4,128)}) custom-call(f32[32,8,256]{2,1,0:T(8,128)} %refs_0_.3, f32[32,8,256]{2,1,0:T(8,128)} %copy-done.1, f32[32,8,256]{2,1,0:T(8,128)} %copy-done, f32[7,8,256]{2,1,0:T(8,128)} %fields.1.refs_3_, f32[7,8,256]{2,1,0:T(8,128)} %copy-done.3, f32[7,8,256]{2,1,0:T(8,128)} %copy-done.2, ...), custom_call_target="tpu_custom_call" | custom-call | tf_op jit(solution)/shard_map/columns/pallas_call | solution.py:305
  39.5 14.5 %all_to_all.5.sums_ref = f32[32,4,128]{2,1,0:T(4,128)} all-to-all(f32[32,4,128]{2,1,0:T(4,128)} %get-tuple-element.8), channel_id=1, replica_groups=mesh['gx'=4,'gy'=8] {'gx','gy'}, dimensions={0} | all-to-all | bytes 131072 | tf_op jit(solution)/shard_map/all_to_all | solution.py:316
  53.9 1.6 %finish.1 = (f32[8,256]{1,0:T(8,128)}, f32[8,256]{1,0:T(8,128)}) custom-call(f32[32,4,128]{2,1,0:T(4,128)} %all_to_all.5.sums_ref, f32[5,8,256]{2,1,0:T(8,128)} %get-tuple-element.9.own_ref, f32[8,256]{1,0:T(8,128)} %warm_start.3), custom_call_target="tpu_custom_call" | custom-call | tf_op jit(solution)/shard_map/finish/pallas_call | solution.py:317
  (5 shorter events, 0.0 us)
Async XLA Ops:
  0.6 18.5 %collective-permute-start.1 = (f32[32,8,256]{2,1,0:T(8,128)}, f32[32,8,256]{2,1,0:T(8,128)S(1)}, u32[]{:S(2)}, u32[]{:S(2)}) collective-permute-start(f32[32,8,256]{2,1,0:T(8,128)} %refs_0_.3), channel_id=1, source_target_pairs={{0,8},{8,16},{16,24},{1,9},{9,17},{17,25},{2,10},{10,18},{18,26},{... | collective-permute-start | bytes 786440 | tf_op jit(solution)/shard_map/ppermute | solution.py:282
  5.6 13.6 %collective-permute-start = (f32[32,8,256]{2,1,0:T(8,128)}, f32[32,8,256]{2,1,0:T(8,128)S(1)}, u32[]{:S(2)}, u32[]{:S(2)}) collective-permute-start(f32[32,8,256]{2,1,0:T(8,128)} %refs_0_.3), channel_id=1, source_target_pairs={{8,0},{16,8},{24,16},{9,1},{17,9},{25,17},{10,2},{18,10},{26,18},{... | collective-permute-start | bytes 786440 | tf_op jit(solution)/shard_map/ppermute | solution.py:281
  8.3 6.7 %collective-permute-start.3 = (f32[7,8,256]{2,1,0:T(8,128)}, f32[7,8,256]{2,1,0:T(8,128)S(1)}, u32[]{:S(2)}, u32[]{:S(2)}) collective-permute-start(f32[7,8,256]{2,1,0:T(8,128)} %fields.1.refs_3_), channel_id=1, source_target_pairs={{0,8},{8,16},{16,24},{1,9},{9,17},{17,25},{2,10},{10,18},{18,26},{... | collective-permute-start | bytes 172040 | tf_op jit(solution)/shard_map/ppermute | solution.py:292
  12.9 6.3 %collective-permute-start.2 = (f32[7,8,256]{2,1,0:T(8,128)}, f32[7,8,256]{2,1,0:T(8,128)S(1)}, u32[]{:S(2)}, u32[]{:S(2)}) collective-permute-start(f32[7,8,256]{2,1,0:T(8,128)} %fields.1.refs_3_), channel_id=1, source_target_pairs={{8,0},{16,8},{24,16},{9,1},{17,9},{25,17},{10,2},{18,10},{26,18},{... | collective-permute-start | bytes 172040 | tf_op jit(solution)/shard_map/ppermute | solution.py:291
  15.0 4.2 %copy-start.2 = (f32[7,8,256]{2,1,0:T(8,128)}, f32[7,8,256]{2,1,0:T(8,128)S(1)}, u32[]{:S(2)}) copy-start(f32[7,8,256]{2,1,0:T(8,128)S(1)} %collective-permute-done.3.refs_5_) | copy-start | bytes 172036
  19.2 0.6 %copy-start.3 = (f32[7,8,256]{2,1,0:T(8,128)}, f32[7,8,256]{2,1,0:T(8,128)S(1)}, u32[]{:S(2)}) copy-start(f32[7,8,256]{2,1,0:T(8,128)S(1)} %collective-permute-done.2.refs_4_) | copy-start | bytes 172036
  19.2 0.7 %copy-start = (f32[32,8,256]{2,1,0:T(8,128)}, f32[32,8,256]{2,1,0:T(8,128)S(1)}, u32[]{:S(2)}) copy-start(f32[32,8,256]{2,1,0:T(8,128)S(1)} %collective-permute-done.1.refs_2_) | copy-start | bytes 786436
  19.9 0.7 %copy-start.1 = (f32[32,8,256]{2,1,0:T(8,128)}, f32[32,8,256]{2,1,0:T(8,128)S(1)}, u32[]{:S(2)}) copy-start(f32[32,8,256]{2,1,0:T(8,128)S(1)} %collective-permute-done.refs_1_) | copy-start | bytes 786436
  22.6 2.6 %collective-permute-start.4 = (f32[24,256]{1,0:T(8,128)}, f32[24,256]{1,0:T(8,128)S(1)}, u32[]{:S(2)}, u32[]{:S(2)}) collective-permute-start(f32[24,256]{1,0:T(8,128)} %get-tuple-element.6), channel_id=1, source_target_pairs={{0,1},{1,2},{2,3},{3,4},{4,5},{5,6},{6,7},{8,9},{9,10},{10,11},{11... | collective-permute-start | bytes 73736 | tf_op jit(solution)/shard_map/ppermute | solution.py:302
  23.9 5.0 %collective-permute-start.5 = (f32[24,256]{1,0:T(8,128)}, f32[24,256]{1,0:T(8,128)S(1)}, u32[]{:S(2)}, u32[]{:S(2)}) collective-permute-start(f32[24,256]{1,0:T(8,128)} %get-tuple-element.7), channel_id=1, source_target_pairs={{1,0},{2,1},{3,2},{4,3},{5,4},{6,5},{7,6},{9,8},{10,9},{11,10},{12... | collective-permute-start | bytes 73736 | tf_op jit(solution)/shard_map/ppermute | solution.py:301
  25.2 3.7 %copy-start.4 = (f32[24,256]{1,0:T(8,128)}, f32[24,256]{1,0:T(8,128)S(1)}, u32[]{:S(2)}) copy-start(f32[24,256]{1,0:T(8,128)S(1)} %collective-permute-done.4.refs_6_) | copy-start | bytes 73732
  29.0 0.6 %copy-start.5 = (f32[24,256]{1,0:T(8,128)}, f32[24,256]{1,0:T(8,128)S(1)}, u32[]{:S(2)}) copy-start(f32[24,256]{1,0:T(8,128)S(1)} %collective-permute-done.5.refs_7_) | copy-start | bytes 73732

commit v3 on v2

--- a/solution.py
+++ b/solution.py
@@ -34,54 +34,76 @@
     return pltpu.roll(block, amount, 1) if amount else block
 
 
-def field_kernel(gradient, warm_start, friction_coef, slide, obs_weight, ice, grounded, out_ref):
+def field_kernel(
+    visc, gradient, warm_start, friction_coef, slide, obs_weight, ice, grounded, *out_refs
+):
+    own_ref, to_low, to_high = out_refs
+    levels, rows, _ = visc.shape
     ice_float = ice[...].astype(jnp.float32)
     ground_float = grounded[...].astype(jnp.float32)
     coef = friction_coef[...]
     source = ice_float * ground_float * coef
-    out_ref[0] = ground_float * coef
-    out_ref[1] = source * slide[0]
-    out_ref[2] = source * slide[1]
-    out_ref[3] = ice_float * obs_weight[...]
-    out_ref[4] = 1.0 / (
+    own_ref[0] = ground_float * coef
+    own_ref[1] = source * slide[0]
+    own_ref[2] = source * slide[1]
+    own_ref[3] = ice_float * obs_weight[...]
+    own_ref[4] = 1.0 / (
         reg_gamma * (1.0 + 4.0 * reg_smooth)
         + diag_scale * ice_float * ground_float * coef * coef
     )
-    out_ref[5] = gradient[...]
-    out_ref[6] = warm_start[...]
-
-
-def pack_kernel(*refs):
-    layers, fields = refs[0:3], refs[3:6]
-    to_low, to_high = refs[6:8]
-    levels, rows, cols = layers[0].shape
+    own_ref[5] = gradient[...]
+    own_ref[6] = warm_start[...]
+    tiles = [visc[z] for z in range(levels)] + [own_ref[z] for z in range(FIELDS)]
+    for z, tile in enumerate(tiles):
+        to_low[HALO * z : HALO * z + rows] = tile
+    for z in range(levels + FIELDS - 1, -1, -1):
+        to_high[HALO * z : HALO * z + rows] = tiles[z]
+
+
+def tiles_of(visc, own, from_low, from_high, z, lanes):
+    levels, rows, _ = visc.shape
+    ref, index = (visc, z) if z < levels else (own, z - levels)
+    band = slice(HALO * z, HALO * z + rows)
+    own_tile, high, low = ref[index, :, lanes], from_high[band, lanes], from_low[band, lanes]
+    row = lax.broadcasted_iota(jnp.int32, own_tile.shape, 0)
+    return (
+        own_tile,
+        jnp.where(row < HALO, high, 0.0),
+        jnp.where(row >= rows - HALO, low, 0.0),
+    )
+
+
+def pack_kernel(visc, own, row_low, row_high, to_low, to_high):
+    levels, rows, cols = visc.shape
     lane = lax.broadcasted_iota(jnp.int32, (rows, LANES), 1)
-    for t in range(3):
-        for group in range(0, levels + FIELDS, SLOTS):
-            first = jnp.zeros((rows, LANES), jnp.float32)
-            last = first
-            for z in range(group, min(group + SLOTS, levels + FIELDS)):
-                ref, index = (layers[t], z) if z < levels else (fields[t], z - levels)
-                at = HALO * (z - group)
-                here = (lane >= at) & (lane < at + HALO)
-                first = jnp.where(here, turned(ref[index, :, :LANES], at), first)
-                shift = at - (LANES - HALO)
-                last = jnp.where(here, turned(ref[index, :, cols - LANES :], shift), last)
-            place = (group // SLOTS) * LANES
-            to_low[t * rows : (t + 1) * rows, place : place + LANES] = first
-            to_high[t * rows : (t + 1) * rows, place : place + LANES] = last
-
-
-def assemble(layers, fields, from_low, from_high, wide_ref):
-    levels, rows, cols = layers[0].shape
+    zero = jnp.zeros((rows, LANES), jnp.float32)
+    for group in range(0, levels + FIELDS, SLOTS):
+        first, last = [zero] * 3, [zero] * 3
+        for z in range(group, min(group + SLOTS, levels + FIELDS)):
+            at = HALO * (z - group)
+            here = (lane >= at) & (lane < at + HALO)
+            shift = at - (LANES - HALO)
+            left = tiles_of(visc, own, row_low, row_high, z, slice(0, LANES))
+            right = tiles_of(visc, own, row_low, row_high, z, slice(cols - LANES, cols))
+            for t in range(3):
+                first[t] = jnp.where(here, turned(left[t], at), first[t])
+                last[t] = jnp.where(here, turned(right[t], shift), last[t])
+        place = (group // SLOTS) * LANES
+        for t in range(3):
+            to_low[t * rows : (t + 1) * rows, place : place + LANES] = first[t]
+            to_high[t * rows : (t + 1) * rows, place : place + LANES] = last[t]
+
+
+def assemble(visc, own, row_low, row_high, from_low, from_high, wide_ref):
+    levels, rows, cols = visc.shape
     lane = lax.broadcasted_iota(jnp.int32, (rows, LANES), 1)
     for z in range(levels + FIELDS):
         at = HALO * (z % SLOTS)
         place = (z // SLOTS) * LANES
+        tiles = tiles_of(visc, own, row_low, row_high, z, slice(0, cols))
         for t in range(3):
-            ref, index = (layers[t], z) if z < levels else (fields[t], z - levels)
             band = slice(t * rows, (t + 1) * rows)
-            wide_ref[z, band, :cols] = ref[index]
+            wide_ref[z, band, :cols] = tiles[t]
             high = turned(from_high[band, place : place + LANES], -at)
             low = turned(from_low[band, place : place + LANES], LANES - HALO - at)
             edge = jnp.where(lane < HALO, high, jnp.where(lane >= LANES - HALO, low, 0.0))
@@ -205,11 +227,10 @@
 
 
 def column_kernel(*refs):
-    layers, fields, (from_low, from_high) = refs[0:3], refs[3:6], refs[6:8]
-    own_ref, sums_ref, wide_ref = refs[8:11]
-    tops, heavy_tops, (bed_ref, heavy_bed) = refs[11:14], refs[14:17], refs[17:19]
-    levels, rows, cols = layers[0].shape
-    assemble(layers, fields, from_low, from_high, wide_ref)
+    own_ref, sums_ref, wide_ref = refs[6:9]
+    tops, heavy_tops, (bed_ref, heavy_bed) = refs[9:12], refs[12:15], refs[15:17]
+    levels, rows, cols = refs[0].shape
+    assemble(*refs[0:6], wide_ref)
     through = vertical(wide_ref, tops, heavy_tops, bed_ref, heavy_bed)
     back = couplings(levels, rows, tops, heavy_tops, bed_ref, heavy_bed)
     forth = {(dx, dy): moved(back[-dx, -dy], dx, dy) for dx, dy in back}
@@ -275,28 +296,20 @@
     gradient, warm_start, viscosity, friction_coef, slide_dir, obs_weight, ice_mask, grounded
 ):
     levels, rows, cols = viscosity.shape
+    sent = jax.ShapeDtypeStruct((-(-(HALO * (levels + FIELDS) + rows) // 8) * 8, cols), jnp.float32)
+    fields, to_low, to_high = pl.pallas_call(
+        field_kernel,
+        out_shape=(jax.ShapeDtypeStruct((FIELDS, rows, cols), jnp.float32), sent, sent),
+        name="fields",
+    )(viscosity, gradient, warm_start, friction_coef, slide_dir, obs_weight, ice_mask, grounded)
     forward, backward = neighbours("gx")
-    layers = (
-        viscosity,
-        lax.ppermute(viscosity, "gx", backward),
-        lax.ppermute(viscosity, "gx", forward),
-    )
-    own_fields = pl.pallas_call(
-        field_kernel,
-        out_shape=jax.ShapeDtypeStruct((FIELDS, rows, cols), jnp.float32),
-        name="fields",
-    )(gradient, warm_start, friction_coef, slide_dir, obs_weight, ice_mask, grounded)
-    fields = (
-        own_fields,
-        lax.ppermute(own_fields, "gx", backward),
-        lax.ppermute(own_fields, "gx", forward),
-    )
+    row_high = lax.ppermute(to_low, "gx", backward)
+    row_low = lax.ppermute(to_high, "gx", forward)
     packed = jax.ShapeDtypeStruct(
         (3 * rows, -(-(levels + FIELDS) // SLOTS) * LANES), jnp.float32
     )
-    to_low, to_high = pl.pallas_call(pack_kernel, out_shape=(packed, packed), name="pack")(
-        *layers, *fields
-    )
+    pieces = (viscosity, fields, row_low, row_high)
+    to_low, to_high = pl.pallas_call(pack_kernel, out_shape=(packed, packed), name="pack")(*pieces)
     forward, backward = neighbours("gy")
     from_high = lax.ppermute(to_low, "gy", backward)
     from_low = lax.ppermute(to_high, "gy", forward)
@@ -312,7 +325,7 @@
         + [pltpu.VMEM((levels,) + span, jnp.float32)] * 6
         + [pltpu.VMEM((levels + 2,) + span, jnp.float32)] * 2,
         name="columns",
-    )(*layers, *fields, from_low, from_high)
+    )(*pieces, from_low, from_high)
     sums = lax.all_to_all(sums, ("gx", "gy"), 0, 0)
     return pl.pallas_call(
         finish_kernel,

time: 56 us -> 53.2 us (0.950)
  starting transfers between devices: 14.7 us -> 8.82 us
  waiting for transfers between devices: 8.69 us -> 12.1 us
  local copies, waits for them, and re-layouts: 2.02 us -> 1.3 us
    ppermute x4 -> x2, starting transfers between devices: 12.1 us -> 6.25 us  [the longest x1 4.96 us: on_device(): row_low = lax.ppermute(to_high, 'gx', forward)]
    ppermute x4 -> x2, waiting for transfers between devices: 4.98 us -> 8.39 us  [the longest x1 4.37 us: on_device(): row_low = lax.ppermute(to_high, 'gx', forward)]
    unnamed x12 -> x8, local copies, waits for them, and re-layouts: 2.02 us -> 1.3 us
  transfers between devices with their start and end apart: 6 -> 4, of which waited for: 3 -> 3; matrix products, arithmetic and copies ran while one was open for 0% -> 0% of each run, Pallas kernels for 3% -> 0%
where the time goes in v3:
time: 53.2 us; the launch traced here: 52.9 us
  Pallas kernels  15.5 us (29%)
  blocking collectives  14.4 us (27%)
  waiting for transfers between devices  12.1 us (23%)
  starting transfers between devices  8.82 us (17%)
  local copies, waits for them, and re-layouts  1.3 us (2%)
  between operations  0.69 us (1%)
    all_to_all x1, blocking collectives, on_device(): sums = lax.all_to_all(sums, ('gx', 'gy'), 0, 0)  14.4 us
    pallas_call x1, Pallas kernels, on_device(): pl.pallas_call(column_kernel, out_shape=(jax.ShapeDtypeStruct((5, rows, c...  9.87 us
    ppermute x1, starting transfers between devices, on_device(): row_low = lax.ppermute(to_high, 'gx', forward)  4.96 us
    ppermute x1, waiting for transfers between devices, on_device(): row_low = lax.ppermute(to_high, 'gx', forward)  4.37 us
    ppermute x1, waiting for transfers between devices, on_device(): row_high = lax.ppermute(to_low, 'gx', backward)  4.02 us
    ppermute x1, waiting for transfers between devices, on_device(): from_high = lax.ppermute(to_low, 'gy', backward)  3.7 us
    pallas_call x1, Pallas kernels, on_device(): pl.pallas_call(pack_kernel, out_shape=(packed, packed), name='pack')  2.11 us
    pallas_call x1, Pallas kernels, on_device(): pl.pallas_call(field_kernel, out_shape=(jax.ShapeDtypeStruct((FIELDS, row...  1.87 us
  transfers between devices with their start and end apart: 4, of which 3 were waited for; matrix products, arithmetic and copies ran while one was open for 0% of the time, Pallas kernels for 0%

profile of v3, /device:TPU:0, one launch (start us, length us, event | category | flops | bytes accessed | tf_op | source)
XLA Modules:
  0.0 52.9 jit_solution(385157974337135891)
XLA Ops:
  0.6 1.9 %fields.1 = (f32[7,8,256]{2,1,0:T(8,128)}, f32[248,256]{1,0:T(8,128)}, f32[248,256]{1,0:T(8,128)}) custom-call(f32[32,8,256]{2,1,0:T(8,128)} %refs_0_.1, f32[8,256]{1,0:T(8,128)} %gradient.1, f32[8,256]{1,0:T(8,128)} %warm_start.3, f32[8,256]{1,0:T(8,128)} %friction_coef.1, f32[2,8,256]{2,1,0:T(8,128)} %slide.1, f32[8,256]{1,0:T(8,128)} %obs_weight.1, ...), custom_call_target="tpu_custom_call" | custom-call | tf_op jit(solution)/shard_map/fields/pallas_call | solution.py:300
  2.5 5.0 %collective-permute-start = (f32[248,256]{1,0:T(8,128)}, f32[248,256]{1,0:T(8,128)S(1)}, u32[]{:S(2)}, u32[]{:S(2)}) collective-permute-start(f32[248,256]{1,0:T(8,128)} %get-tuple-element.10), channel_id=1, source_target_pairs={{0,8},{8,16},{16,24},{1,9},{9,17},{17,25},{2,10},{10,18},{18,26},{... | collective-permute-start | bytes 761864 | tf_op jit(solution)/shard_map/ppermute | solution.py:307
  7.5 1.3 %collective-permute-start.1 = (f32[248,256]{1,0:T(8,128)}, f32[248,256]{1,0:T(8,128)S(1)}, u32[]{:S(2)}, u32[]{:S(2)}) collective-permute-start(f32[248,256]{1,0:T(8,128)} %get-tuple-element.11), channel_id=1, source_target_pairs={{8,0},{16,8},{24,16},{9,1},{17,9},{25,17},{10,2},{18,10},{26,18},{... | collective-permute-start | bytes 761864 | tf_op jit(solution)/shard_map/ppermute | solution.py:306
  8.8 4.4 %collective-permute-done.row_low.refs_2_ = f32[248,256]{1,0:T(8,128)S(1)} collective-permute-done((f32[248,256]{1,0:T(8,128)}, f32[248,256]{1,0:T(8,128)S(1)}, u32[]{:S(2)}, u32[]{:S(2)}) %collective-permute-start) | collective-permute-done | bytes 253984 | tf_op jit(solution)/shard_map/ppermute | solution.py:307
  13.1 0.0 copy-start
  13.1 4.0 %collective-permute-done.1.row_high.refs_3_ = f32[248,256]{1,0:T(8,128)S(1)} collective-permute-done((f32[248,256]{1,0:T(8,128)}, f32[248,256]{1,0:T(8,128)S(1)}, u32[]{:S(2)}, u32[]{:S(2)}) %collective-permute-start.1) | collective-permute-done | bytes 253984 | tf_op jit(solution)/shard_map/ppermute | solution.py:306
  17.2 0.0 copy-start.1
  17.2 0.0 copy-done
  17.2 0.7 %copy-done.1 = f32[248,256]{1,0:T(8,128)} copy-done((f32[248,256]{1,0:T(8,128)}, f32[248,256]{1,0:T(8,128)S(1)}, u32[]{:S(2)}) %copy-start.1) | copy-done | bytes 253976
  17.9 2.1 %pack.1 = (f32[24,256]{1,0:T(8,128)}, f32[24,256]{1,0:T(8,128)}) custom-call(f32[32,8,256]{2,1,0:T(8,128)} %refs_0_.1, f32[7,8,256]{2,1,0:T(8,128)} %get-tuple-element.9.own.refs_1_, f32[248,256]{1,0:T(8,128)} %copy-done, f32[248,256]{1,0:T(8,128)} %copy-done.1), custom_call_target="tpu_custom_call" | custom-call | tf_op jit(solution)/shard_map/pack/pallas_call | solution.py:312
  20.0 1.3 %collective-permute-start.2 = (f32[24,256]{1,0:T(8,128)}, f32[24,256]{1,0:T(8,128)S(1)}, u32[]{:S(2)}, u32[]{:S(2)}) collective-permute-start(f32[24,256]{1,0:T(8,128)} %get-tuple-element.12), channel_id=1, source_target_pairs={{0,1},{1,2},{2,3},{3,4},{4,5},{5,6},{6,7},{8,9},{9,10},{10,11},{11... | collective-permute-start | bytes 73736 | tf_op jit(solution)/shard_map/ppermute | solution.py:315
  21.3 1.3 %collective-permute-start.3 = (f32[24,256]{1,0:T(8,128)}, f32[24,256]{1,0:T(8,128)S(1)}, u32[]{:S(2)}, u32[]{:S(2)}) collective-permute-start(f32[24,256]{1,0:T(8,128)} %get-tuple-element.13), channel_id=1, source_target_pairs={{1,0},{2,1},{3,2},{4,3},{5,4},{6,5},{7,6},{9,8},{10,9},{11,10},{12... | collective-permute-start | bytes 73736 | tf_op jit(solution)/shard_map/ppermute | solution.py:314
  22.6 0.0 collective-permute-done.2.refs_4_
  22.6 0.0 copy-start.2
  22.6 3.7 %collective-permute-done.3.refs_5_ = f32[24,256]{1,0:T(8,128)S(1)} collective-permute-done((f32[24,256]{1,0:T(8,128)}, f32[24,256]{1,0:T(8,128)S(1)}, u32[]{:S(2)}, u32[]{:S(2)}) %collective-permute-start.3) | collective-permute-done | bytes 24608 | tf_op jit(solution)/shard_map/ppermute | solution.py:314
  26.3 0.0 copy-done.2
  26.3 0.0 copy-start.3
  26.3 0.6 %copy-done.3 = f32[24,256]{1,0:T(8,128)} copy-done((f32[24,256]{1,0:T(8,128)}, f32[24,256]{1,0:T(8,128)S(1)}, u32[]{:S(2)}) %copy-start.3) | copy-done | bytes 24600
  26.9 9.9 %columns.1 = (f32[5,8,256]{2,1,0:T(8,128)}, f32[32,4,128]{2,1,0:T(4,128)}) custom-call(f32[32,8,256]{2,1,0:T(8,128)} %refs_0_.1, f32[7,8,256]{2,1,0:T(8,128)} %get-tuple-element.9.own.refs_1_, f32[248,256]{1,0:T(8,128)} %copy-done, f32[248,256]{1,0:T(8,128)} %copy-done.1, f32[24,256]{1,0:T(8,128)} %copy-done.2, f32[24,256]{1,0:T(8,128)} %copy-done.3), custom_call_target="tpu_custom_call" | custom-call | tf_op jit(solution)/shard_map/columns/pallas_call | solution.py:318
  36.8 14.4 %all_to_all.5.sums_ref = f32[32,4,128]{2,1,0:T(4,128)} all-to-all(f32[32,4,128]{2,1,0:T(4,128)} %get-tuple-element.14), channel_id=1, replica_groups=mesh['gx'=4,'gy'=8] {'gx','gy'}, dimensions={0} | all-to-all | bytes 131072 | tf_op jit(solution)/shard_map/all_to_all | solution.py:329
  51.2 1.6 %finish.1 = (f32[8,256]{1,0:T(8,128)}, f32[8,256]{1,0:T(8,128)}) custom-call(f32[32,4,128]{2,1,0:T(4,128)} %all_to_all.5.sums_ref, f32[5,8,256]{2,1,0:T(8,128)} %get-tuple-element.15.own_ref, f32[8,256]{1,0:T(8,128)} %warm_start.3), custom_call_target="tpu_custom_call" | custom-call | tf_op jit(solution)/shard_map/finish/pallas_call | solution.py:330
Async XLA Ops:
  2.5 10.6 %collective-permute-start = (f32[248,256]{1,0:T(8,128)}, f32[248,256]{1,0:T(8,128)S(1)}, u32[]{:S(2)}, u32[]{:S(2)}) collective-permute-start(f32[248,256]{1,0:T(8,128)} %get-tuple-element.10), channel_id=1, source_target_pairs={{0,8},{8,16},{16,24},{1,9},{9,17},{17,25},{2,10},{10,18},{18,26},{... | collective-permute-start | bytes 761864 | tf_op jit(solution)/shard_map/ppermute | solution.py:307
  7.5 9.7 %collective-permute-start.1 = (f32[248,256]{1,0:T(8,128)}, f32[248,256]{1,0:T(8,128)S(1)}, u32[]{:S(2)}, u32[]{:S(2)}) collective-permute-start(f32[248,256]{1,0:T(8,128)} %get-tuple-element.11), channel_id=1, source_target_pairs={{8,0},{16,8},{24,16},{9,1},{17,9},{25,17},{10,2},{18,10},{26,18},{... | collective-permute-start | bytes 761864 | tf_op jit(solution)/shard_map/ppermute | solution.py:306
  13.1 4.0 %copy-start = (f32[248,256]{1,0:T(8,128)}, f32[248,256]{1,0:T(8,128)S(1)}, u32[]{:S(2)}) copy-start(f32[248,256]{1,0:T(8,128)S(1)} %collective-permute-done.row_low.refs_2_) | copy-start | bytes 761860
  17.2 0.7 %copy-start.1 = (f32[248,256]{1,0:T(8,128)}, f32[248,256]{1,0:T(8,128)S(1)}, u32[]{:S(2)}) copy-start(f32[248,256]{1,0:T(8,128)S(1)} %collective-permute-done.1.row_high.refs_3_) | copy-start | bytes 761860
  20.0 2.6 %collective-permute-start.2 = (f32[24,256]{1,0:T(8,128)}, f32[24,256]{1,0:T(8,128)S(1)}, u32[]{:S(2)}, u32[]{:S(2)}) collective-permute-start(f32[24,256]{1,0:T(8,128)} %get-tuple-element.12), channel_id=1, source_target_pairs={{0,1},{1,2},{2,3},{3,4},{4,5},{5,6},{6,7},{8,9},{9,10},{10,11},{11... | collective-permute-start | bytes 73736 | tf_op jit(solution)/shard_map/ppermute | solution.py:315
  21.3 5.0 %collective-permute-start.3 = (f32[24,256]{1,0:T(8,128)}, f32[24,256]{1,0:T(8,128)S(1)}, u32[]{:S(2)}, u32[]{:S(2)}) collective-permute-start(f32[24,256]{1,0:T(8,128)} %get-tuple-element.13), channel_id=1, source_target_pairs={{1,0},{2,1},{3,2},{4,3},{5,4},{6,5},{7,6},{9,8},{10,9},{11,10},{12... | collective-permute-start | bytes 73736 | tf_op jit(solution)/shard_map/ppermute | solution.py:314
  22.6 3.7 %copy-start.2 = (f32[24,256]{1,0:T(8,128)}, f32[24,256]{1,0:T(8,128)S(1)}, u32[]{:S(2)}) copy-start(f32[24,256]{1,0:T(8,128)S(1)} %collective-permute-done.2.refs_4_) | copy-start | bytes 73732
  26.3 0.6 %copy-start.3 = (f32[24,256]{1,0:T(8,128)}, f32[24,256]{1,0:T(8,128)S(1)}, u32[]{:S(2)}) copy-start(f32[24,256]{1,0:T(8,128)S(1)} %collective-permute-done.3.refs_5_) | copy-start | bytes 73732

commit v4 on v3

--- a/solution.py
+++ b/solution.py
@@ -37,8 +37,8 @@
 def field_kernel(
     visc, gradient, warm_start, friction_coef, slide, obs_weight, ice, grounded, *out_refs
 ):
-    own_ref, to_low, to_high = out_refs
-    levels, rows, _ = visc.shape
+    own_ref, to_low, to_high, first_ref, last_ref = out_refs
+    levels, rows, cols = visc.shape
     ice_float = ice[...].astype(jnp.float32)
     ground_float = grounded[...].astype(jnp.float32)
     coef = friction_coef[...]
@@ -58,6 +58,19 @@
         to_low[HALO * z : HALO * z + rows] = tile
     for z in range(levels + FIELDS - 1, -1, -1):
         to_high[HALO * z : HALO * z + rows] = tiles[z]
+    lane = lax.broadcasted_iota(jnp.int32, (rows, LANES), 1)
+    for group in range(0, levels + FIELDS, SLOTS):
+        first = jnp.zeros((rows, LANES), jnp.float32)
+        last = first
+        for z in range(group, min(group + SLOTS, levels + FIELDS)):
+            at = HALO * (z - group)
+            here = (lane >= at) & (lane < at + HALO)
+            first = jnp.where(here, turned(tiles[z][:, :LANES], at), first)
+            shift = at - (LANES - HALO)
+            last = jnp.where(here, turned(tiles[z][:, cols - LANES :], shift), last)
+        place = (group // SLOTS) * LANES
+        first_ref[:, place : place + LANES] = first
+        last_ref[:, place : place + LANES] = last
 
 
 def tiles_of(visc, own, from_low, from_high, z, lanes):
@@ -73,28 +86,7 @@
     )
 
 
-def pack_kernel(visc, own, row_low, row_high, to_low, to_high):
-    levels, rows, cols = visc.shape
-    lane = lax.broadcasted_iota(jnp.int32, (rows, LANES), 1)
-    zero = jnp.zeros((rows, LANES), jnp.float32)
-    for group in range(0, levels + FIELDS, SLOTS):
-        first, last = [zero] * 3, [zero] * 3
-        for z in range(group, min(group + SLOTS, levels + FIELDS)):
-            at = HALO * (z - group)
-            here = (lane >= at) & (lane < at + HALO)
-            shift = at - (LANES - HALO)
-            left = tiles_of(visc, own, row_low, row_high, z, slice(0, LANES))
-            right = tiles_of(visc, own, row_low, row_high, z, slice(cols - LANES, cols))
-            for t in range(3):
-                first[t] = jnp.where(here, turned(left[t], at), first[t])
-                last[t] = jnp.where(here, turned(right[t], shift), last[t])
-        place = (group // SLOTS) * LANES
-        for t in range(3):
-            to_low[t * rows : (t + 1) * rows, place : place + LANES] = first[t]
-            to_high[t * rows : (t + 1) * rows, place : place + LANES] = last[t]
-
-
-def assemble(visc, own, row_low, row_high, from_low, from_high, wide_ref):
+def assemble(visc, own, row_low, row_high, edges, wide_ref):
     levels, rows, cols = visc.shape
     lane = lax.broadcasted_iota(jnp.int32, (rows, LANES), 1)
     for z in range(levels + FIELDS):
@@ -104,8 +96,8 @@
         for t in range(3):
             band = slice(t * rows, (t + 1) * rows)
             wide_ref[z, band, :cols] = tiles[t]
-            high = turned(from_high[band, place : place + LANES], -at)
-            low = turned(from_low[band, place : place + LANES], LANES - HALO - at)
+            low = turned(edges[t][0, :, place : place + LANES], LANES - HALO - at)
+            high = turned(edges[t][1, :, place : place + LANES], -at)
             edge = jnp.where(lane < HALO, high, jnp.where(lane >= LANES - HALO, low, 0.0))
             wide_ref[z, band, cols:] = edge
 
@@ -227,10 +219,10 @@
 
 
 def column_kernel(*refs):
-    own_ref, sums_ref, wide_ref = refs[6:9]
-    tops, heavy_tops, (bed_ref, heavy_bed) = refs[9:12], refs[12:15], refs[15:17]
+    own_ref, sums_ref, wide_ref = refs[7:10]
+    tops, heavy_tops, (bed_ref, heavy_bed) = refs[10:13], refs[13:16], refs[16:18]
     levels, rows, cols = refs[0].shape
-    assemble(*refs[0:6], wide_ref)
+    assemble(*refs[0:4], refs[4:7], wide_ref)
     through = vertical(wide_ref, tops, heavy_tops, bed_ref, heavy_bed)
     back = couplings(levels, rows, tops, heavy_tops, bed_ref, heavy_bed)
     forth = {(dx, dy): moved(back[-dx, -dy], dx, dy) for dx, dy in back}
@@ -297,22 +289,31 @@
 ):
     levels, rows, cols = viscosity.shape
     sent = jax.ShapeDtypeStruct((-(-(HALO * (levels + FIELDS) + rows) // 8) * 8, cols), jnp.float32)
-    fields, to_low, to_high = pl.pallas_call(
+    packed = jax.ShapeDtypeStruct((rows, -(-(levels + FIELDS) // SLOTS) * LANES), jnp.float32)
+    fields, to_low, to_high, first, last = pl.pallas_call(
         field_kernel,
-        out_shape=(jax.ShapeDtypeStruct((FIELDS, rows, cols), jnp.float32), sent, sent),
+        out_shape=(
+            jax.ShapeDtypeStruct((FIELDS, rows, cols), jnp.float32),
+            sent,
+            sent,
+            packed,
+            packed,
+        ),
         name="fields",
     )(viscosity, gradient, warm_start, friction_coef, slide_dir, obs_weight, ice_mask, grounded)
-    forward, backward = neighbours("gx")
-    row_high = lax.ppermute(to_low, "gx", backward)
-    row_low = lax.ppermute(to_high, "gx", forward)
-    packed = jax.ShapeDtypeStruct(
-        (3 * rows, -(-(levels + FIELDS) // SLOTS) * LANES), jnp.float32
+    next_x, previous_x = neighbours("gx")[::-1]
+    next_y, previous_y = neighbours("gy")[::-1]
+    row_high = lax.ppermute(to_low, "gx", next_x)
+    row_low = lax.ppermute(to_high, "gx", previous_x)
+    edges = jnp.stack(
+        [lax.ppermute(last, "gy", previous_y), lax.ppermute(first, "gy", next_y)]
+    )
+    edges = (
+        edges,
+        lax.ppermute(edges, "gx", next_x),
+        lax.ppermute(edges, "gx", previous_x),
     )
     pieces = (viscosity, fields, row_low, row_high)
-    to_low, to_high = pl.pallas_call(pack_kernel, out_shape=(packed, packed), name="pack")(*pieces)
-    forward, backward = neighbours("gy")
-    from_high = lax.ppermute(to_low, "gy", backward)
-    from_low = lax.ppermute(to_high, "gy", forward)
     devices = lax.axis_size("gx") * lax.axis_size("gy")
     span = (3 * rows, cols + LANES)
     own, sums = pl.pallas_call(
@@ -325,7 +326,7 @@
         + [pltpu.VMEM((levels,) + span, jnp.float32)] * 6
         + [pltpu.VMEM((levels + 2,) + span, jnp.float32)] * 2,
         name="columns",
-    )(*pieces, from_low, from_high)
+    )(*pieces, *edges)
     sums = lax.all_to_all(sums, ("gx", "gy"), 0, 0)
     return pl.pallas_call(
         finish_kernel,

time: 53.2 us -> 51.3 us (0.964)
  waiting for transfers between devices: 12.1 us -> 2.43 us
  starting transfers between devices: 8.82 us -> 17 us
  blocking collectives: 14.4 us -> 16.5 us
  Pallas kernels: 15.5 us -> 13.5 us
    ppermute x4 -> x6, waiting for transfers between devices: 12.1 us -> 2.43 us  [the longest x1 1.4 us: on_device(): lax.ppermute(edges, 'gx', previous_x)]
    ppermute x4 -> x6, starting transfers between devices: 8.82 us -> 17 us  [the longest x1 5.17 us: on_device(): lax.ppermute(edges, 'gx', previous_x)]
    pallas_call x1 -> x0, Pallas kernels: 2.11 us -> none  [on_device(): pl.pallas_call(pack_kernel, out_shape=(packed, packed), name='pack')]
    all_to_all x1, blocking collectives: 14.4 us -> 16.5 us  [on_device(): sums = lax.all_to_all(sums, ('gx', 'gy'), 0, 0)]
    unnamed x8 -> x10, local copies, waits for them, and re-layouts: 1.3 us -> 0.77 us
  transfers between devices with their start and end apart: 4 -> 6, of which waited for: 3 -> 2; matrix products, arithmetic and copies ran while one was open for 0% -> 0% of each run, Pallas kernels for 0% -> 0%
where the time goes in v4:
time: 51.3 us; the launch traced here: 51 us
  starting transfers between devices  17 us (33%)
  blocking collectives  16.5 us (32%)
  Pallas kernels  13.5 us (26%)
  waiting for transfers between devices  2.43 us (5%)
  local copies, waits for them, and re-layouts  0.77 us (2%)
  between operations  0.74 us (1%)
    all_to_all x1, blocking collectives, on_device(): sums = lax.all_to_all(sums, ('gx', 'gy'), 0, 0)  16.5 us
    pallas_call x1, Pallas kernels, on_device(): pl.pallas_call(column_kernel, out_shape=(jax.ShapeDtypeStruct((5, rows, c...  9.91 us
    ppermute x1, starting transfers between devices, on_device(): lax.ppermute(edges, 'gx', previous_x)  5.17 us
    ppermute x1, starting transfers between devices, on_device(): row_low = lax.ppermute(to_high, 'gx', previous_x)  4.96 us
    ppermute x1, starting transfers between devices, on_device(): lax.ppermute(last, 'gy', previous_y)  3.03 us
    pallas_call x1, Pallas kernels, on_device(): pl.pallas_call(field_kernel, out_shape=(jax.ShapeDtypeStruct((FIELDS, row...  1.91 us
    pallas_call x1, Pallas kernels, on_device(): pl.pallas_call(finish_kernel, out_shape=(jax.ShapeDtypeStruct((rows, cols...  1.64 us
    ppermute x1, waiting for transfers between devices, on_device(): lax.ppermute(edges, 'gx', previous_x)  1.4 us
  transfers between devices with their start and end apart: 6, of which 2 were waited for; matrix products, arithmetic and copies ran while one was open for 0% of the time, Pallas kernels for 0%

profile of v4, /device:TPU:0, one launch (start us, length us, event | category | flops | bytes accessed | tf_op | source)
XLA Modules:
  0.0 51.0 jit_solution(1351516426187009839)
XLA Ops:
  0.6 1.9 %fields.1 = (f32[7,8,256]{2,1,0:T(8,128)}, f32[248,256]{1,0:T(8,128)}, f32[248,256]{1,0:T(8,128)}, f32[8,256]{1,0:T(8,128)}, f32[8,256]{1,0:T(8,128)}) custom-call(f32[32,8,256]{2,1,0:T(8,128)} %refs_0_.1, f32[8,256]{1,0:T(8,128)} %gradient.1, f32[8,256]{1,0:T(8,128)} %warm_start.3, f32[8,256]{1,0:T(8,128)} %friction_coef.1, f32[2,8,256]{2,1,0:T(8,128)} %slide.1, ...), custom_call_target="tpu_custom_call" | custom-call | tf_op jit(solution)/shard_map/fields/pallas_call | solution.py:293
  2.5 5.0 %collective-permute-start = (f32[248,256]{1,0:T(8,128)}, f32[248,256]{1,0:T(8,128)S(1)}, u32[]{:S(2)}, u32[]{:S(2)}) collective-permute-start(f32[248,256]{1,0:T(8,128)} %get-tuple-element.10), channel_id=1, source_target_pairs={{0,8},{8,16},{16,24},{1,9},{9,17},{17,25},{2,10},{10,18},{18,26},{... | collective-permute-start | bytes 761864 | tf_op jit(solution)/shard_map/ppermute | solution.py:307
  7.5 1.3 %collective-permute-start.1 = (f32[248,256]{1,0:T(8,128)}, f32[248,256]{1,0:T(8,128)S(1)}, u32[]{:S(2)}, u32[]{:S(2)}) collective-permute-start(f32[248,256]{1,0:T(8,128)} %get-tuple-element.11), channel_id=1, source_target_pairs={{8,0},{16,8},{24,16},{9,1},{17,9},{25,17},{10,2},{18,10},{26,18},{... | collective-permute-start | bytes 761864 | tf_op jit(solution)/shard_map/ppermute | solution.py:306
  8.8 1.3 %collective-permute-start.3 = (f32[8,256]{1,0:T(8,128)}, f32[8,256]{1,0:T(8,128)S(1)}, u32[]{:S(2)}, u32[]{:S(2)}) collective-permute-start(f32[8,256]{1,0:T(8,128)} %get-tuple-element.13), channel_id=1, source_target_pairs={{1,0},{2,1},{3,2},{4,3},{5,4},{6,5},{7,6},{9,8},{10,9},{11,10},{12... | collective-permute-start | bytes 24584 | tf_op jit(solution)/shard_map/ppermute | solution.py:309
  10.1 3.0 %collective-permute-start.2 = (f32[8,256]{1,0:T(8,128)}, f32[8,256]{1,0:T(8,128)S(1)}, u32[]{:S(2)}, u32[]{:S(2)}) collective-permute-start(f32[8,256]{1,0:T(8,128)} %get-tuple-element.12), channel_id=1, source_target_pairs={{0,1},{1,2},{2,3},{3,4},{4,5},{5,6},{6,7},{8,9},{9,10},{10,11},{11... | collective-permute-start | bytes 24584 | tf_op jit(solution)/shard_map/ppermute | solution.py:309
  13.1 0.0 collective-permute-done.3
  13.2 1.0 %collective-permute-done.2 = f32[8,256]{1,0:T(8,128)S(1)} collective-permute-done((f32[8,256]{1,0:T(8,128)}, f32[8,256]{1,0:T(8,128)S(1)}, u32[]{:S(2)}, u32[]{:S(2)}) %collective-permute-start.2) | collective-permute-done | bytes 8224 | tf_op jit(solution)/shard_map/ppermute | solution.py:309
  14.2 0.0 copy-start.2
  14.2 1.3 %collective-permute-start.4 = (f32[2,8,256]{2,1,0:T(8,128)S(1)}, f32[2,8,256]{2,1,0:T(8,128)S(1)}, u32[]{:S(2)}, u32[]{:S(2)}) collective-permute-start(f32[2,8,256]{2,1,0:T(8,128)S(1)} %pad_maximum_fusion.refs_4_), channel_id=1, source_target_pairs={{8,0},{16,8},{24,16},{9,1},{17,9},{25,17},{10,2},{18,10},{26,18},{... | collective-permute-start | bytes 49160 | tf_op jit(solution)/shard_map/ppermute | solution.py:313
  15.5 5.2 %collective-permute-start.5 = (f32[2,8,256]{2,1,0:T(8,128)S(1)}, f32[2,8,256]{2,1,0:T(8,128)S(1)}, u32[]{:S(2)}, u32[]{:S(2)}) collective-permute-start(f32[2,8,256]{2,1,0:T(8,128)S(1)} %pad_maximum_fusion.refs_4_), channel_id=1, source_target_pairs={{0,8},{8,16},{16,24},{1,9},{9,17},{17,25},{2,10},{10,18},{18,26},{... | collective-permute-start | bytes 49160 | tf_op jit(solution)/shard_map/ppermute | solution.py:314
  20.6 0.0 collective-permute-done.4.refs_5_
  20.7 0.0 copy-start.3
  20.7 1.4 %collective-permute-done.5.refs_6_ = f32[2,8,256]{2,1,0:T(8,128)S(1)} collective-permute-done((f32[2,8,256]{2,1,0:T(8,128)S(1)}, f32[2,8,256]{2,1,0:T(8,128)S(1)}, u32[]{:S(2)}, u32[]{:S(2)}) %collective-permute-start.5) | collective-permute-done | bytes 16416 | tf_op jit(solution)/shard_map/ppermute | solution.py:314
  22.1 0.0 collective-permute-done.refs_2_
  22.1 0.0 collective-permute-done.1.refs_3_
  22.1 0.0 copy-start.1
  22.1 0.0 copy-done.2
  22.1 0.0 copy-done.3
  22.1 0.6 %copy-done.4 = f32[2,8,256]{2,1,0:T(8,128)} copy-done((f32[2,8,256]{2,1,0:T(8,128)}, f32[2,8,256]{2,1,0:T(8,128)S(1)}, u32[]{:S(2)}) %copy-start.4) | copy-done | bytes 16408
  22.7 0.1 copy-done
  22.8 0.1 copy-done.1
  22.9 9.9 %columns.1 = (f32[5,8,256]{2,1,0:T(8,128)}, f32[32,4,128]{2,1,0:T(4,128)}) custom-call(f32[32,8,256]{2,1,0:T(8,128)} %refs_0_.1, f32[7,8,256]{2,1,0:T(8,128)} %get-tuple-element.9.refs_1_, f32[248,256]{1,0:T(8,128)} %copy-done, f32[248,256]{1,0:T(8,128)} %copy-done.1, f32[2,8,256]{2,1,0:T(8,128)} %copy-done.2, f32[2,8,256]{2,1,0:T(8,128)} %copy-done.3, ...), custom_call_target="tpu_custom_call" | custom-call | tf_op jit(solution)/shard_map/columns/pallas_call | solution.py:319
  32.8 16.5 %all_to_all.5.sums_ref = f32[32,4,128]{2,1,0:T(4,128)} all-to-all(f32[32,4,128]{2,1,0:T(4,128)} %get-tuple-element.14), channel_id=1, replica_groups=mesh['gx'=4,'gy'=8] {'gx','gy'}, dimensions={0} | all-to-all | bytes 131072 | tf_op jit(solution)/shard_map/all_to_all | solution.py:330
  49.3 1.6 %finish.1 = (f32[8,256]{1,0:T(8,128)}, f32[8,256]{1,0:T(8,128)}) custom-call(f32[32,4,128]{2,1,0:T(4,128)} %all_to_all.5.sums_ref, f32[5,8,256]{2,1,0:T(8,128)} %get-tuple-element.15.own_ref, f32[8,256]{1,0:T(8,128)} %warm_start.3), custom_call_target="tpu_custom_call" | custom-call | tf_op jit(solution)/shard_map/finish/pallas_call | solution.py:331
  (3 shorter events, 0.0 us)
Async XLA Ops:
  2.5 19.5 %collective-permute-start = (f32[248,256]{1,0:T(8,128)}, f32[248,256]{1,0:T(8,128)S(1)}, u32[]{:S(2)}, u32[]{:S(2)}) collective-permute-start(f32[248,256]{1,0:T(8,128)} %get-tuple-element.10), channel_id=1, source_target_pairs={{0,8},{8,16},{16,24},{1,9},{9,17},{17,25},{2,10},{10,18},{18,26},{... | collective-permute-start | bytes 761864 | tf_op jit(solution)/shard_map/ppermute | solution.py:307
  7.5 14.6 %collective-permute-start.1 = (f32[248,256]{1,0:T(8,128)}, f32[248,256]{1,0:T(8,128)S(1)}, u32[]{:S(2)}, u32[]{:S(2)}) collective-permute-start(f32[248,256]{1,0:T(8,128)} %get-tuple-element.11), channel_id=1, source_target_pairs={{8,0},{16,8},{24,16},{9,1},{17,9},{25,17},{10,2},{18,10},{26,18},{... | collective-permute-start | bytes 761864 | tf_op jit(solution)/shard_map/ppermute | solution.py:306
  8.8 4.3 %collective-permute-start.3 = (f32[8,256]{1,0:T(8,128)}, f32[8,256]{1,0:T(8,128)S(1)}, u32[]{:S(2)}, u32[]{:S(2)}) collective-permute-start(f32[8,256]{1,0:T(8,128)} %get-tuple-element.13), channel_id=1, source_target_pairs={{1,0},{2,1},{3,2},{4,3},{5,4},{6,5},{7,6},{9,8},{10,9},{11,10},{12... | collective-permute-start | bytes 24584 | tf_op jit(solution)/shard_map/ppermute | solution.py:309
  10.1 4.1 %collective-permute-start.2 = (f32[8,256]{1,0:T(8,128)}, f32[8,256]{1,0:T(8,128)S(1)}, u32[]{:S(2)}, u32[]{:S(2)}) collective-permute-start(f32[8,256]{1,0:T(8,128)} %get-tuple-element.12), channel_id=1, source_target_pairs={{0,1},{1,2},{2,3},{3,4},{4,5},{5,6},{6,7},{8,9},{9,10},{10,11},{11... | collective-permute-start | bytes 24584 | tf_op jit(solution)/shard_map/ppermute | solution.py:309
  14.2 7.9 %copy-start.2 = (f32[2,8,256]{2,1,0:T(8,128)}, f32[2,8,256]{2,1,0:T(8,128)S(1)}, u32[]{:S(2)}) copy-start(f32[2,8,256]{2,1,0:T(8,128)S(1)} %pad_maximum_fusion.refs_4_) | copy-start | bytes 49156
  14.2 6.5 %collective-permute-start.4 = (f32[2,8,256]{2,1,0:T(8,128)S(1)}, f32[2,8,256]{2,1,0:T(8,128)S(1)}, u32[]{:S(2)}, u32[]{:S(2)}) collective-permute-start(f32[2,8,256]{2,1,0:T(8,128)S(1)} %pad_maximum_fusion.refs_4_), channel_id=1, source_target_pairs={{8,0},{16,8},{24,16},{9,1},{17,9},{25,17},{10,2},{18,10},{26,18},{... | collective-permute-start | bytes 49160 | tf_op jit(solution)/shard_map/ppermute | solution.py:313
  15.5 6.6 %collective-permute-start.5 = (f32[2,8,256]{2,1,0:T(8,128)S(1)}, f32[2,8,256]{2,1,0:T(8,128)S(1)}, u32[]{:S(2)}, u32[]{:S(2)}) collective-permute-start(f32[2,8,256]{2,1,0:T(8,128)S(1)} %pad_maximum_fusion.refs_4_), channel_id=1, source_target_pairs={{0,8},{8,16},{16,24},{1,9},{9,17},{17,25},{2,10},{10,18},{18,26},{... | collective-permute-start | bytes 49160 | tf_op jit(solution)/shard_map/ppermute | solution.py:314
  20.7 1.5 %copy-start.3 = (f32[2,8,256]{2,1,0:T(8,128)}, f32[2,8,256]{2,1,0:T(8,128)S(1)}, u32[]{:S(2)}) copy-start(f32[2,8,256]{2,1,0:T(8,128)S(1)} %collective-permute-done.4.refs_5_) | copy-start | bytes 49156
  22.1 0.6 %copy-start.4 = (f32[2,8,256]{2,1,0:T(8,128)}, f32[2,8,256]{2,1,0:T(8,128)S(1)}, u32[]{:S(2)}) copy-start(f32[2,8,256]{2,1,0:T(8,128)S(1)} %collective-permute-done.5.refs_6_) | copy-start | bytes 49156
  22.1 0.7 %copy-start = (f32[248,256]{1,0:T(8,128)}, f32[248,256]{1,0:T(8,128)S(1)}, u32[]{:S(2)}) copy-start(f32[248,256]{1,0:T(8,128)S(1)} %collective-permute-done.refs_2_) | copy-start | bytes 761860
  22.1 0.8 %copy-start.1 = (f32[248,256]{1,0:T(8,128)}, f32[248,256]{1,0:T(8,128)S(1)}, u32[]{:S(2)}) copy-start(f32[248,256]{1,0:T(8,128)S(1)} %collective-permute-done.1.refs_3_) | copy-start | bytes 761860
